TPU v7x, 32 devices: a whole 2x2x4 slice. The times are simulated.
32 devices in a mesh: loc: 8 (over y, x, core), stream: 4 (over z).
Axes of the slice: x: 2, y: 2, z: 4, core: 2. Of those that a mesh axis runs over, the one named last changes fastest.
Arguments:
- latent: bfloat16 [12288, 1024], P(('loc', 'stream')), may hold values from -7 to 7
- observations: bfloat16 [4, 8, 8, 32, 1024], P('stream', 'loc'), may hold values from -7 to 7
- counts: int32 [4, 8, 8], P('stream', 'loc'), may hold values from 1 to 32, as said below
- cross_query: bfloat16 [1024, 1024], replicated, may hold values from -1 to 1
- cross_kv: bfloat16 [1024, 2048], replicated, may hold values from -1 to 1
- cross_out: bfloat16 [1024, 1024], replicated, may hold values from -0.1875 to 0.1875
- self_qkv: bfloat16 [1024, 3072], replicated, may hold values from -1 to 1
- self_out: bfloat16 [1024, 1024], replicated, may hold values from -0.1875 to 0.1875
- mlp_in: bfloat16 [1024, 4096], P(None, ('loc', 'stream')), may hold values from -0.1875 to 0.1875
- mlp_out: bfloat16 [1024, 4096], P(None, ('loc', 'stream')), may hold values from -0.09375 to 0.09375
Outputs:
- forecast: bfloat16 [12288, 1024], P(('loc', 'stream'))
Inputs may be any that keep to these rules, and one draw needn't show every extreme that they name: `counts`: slots 0 to count - 1 of a block hold observations and the rest are padding; for every stream some section receives 32 rows from every ingest shard.
All inputs are finite; a program needn't handle non-finite values.
Results may differ from a plain program's by a relative error of at most 0.013.
Values may be sent and summed in bfloat16 or wider, within the bound.
No kernel may reach another device: no remote copies, remote signals or barrier semaphores. Data moves between devices by JAX's collectives and lax.ppermute only.
A program may use at most 192 MiB of HBM per device.

v0:
```python
import functools
import math

import jax
import jax.numpy as jnp
from jax import lax
from jax.experimental import pallas as pl
from jax.experimental.pallas import tpu as pltpu
from jax.sharding import PartitionSpec as P


HEADS = 16
WIN = 512

EPSILON = 1e-06
MASKED = -1e30
LANES = 128
ROWS = 128
SCORES = 1 << 19


F32 = jnp.float32
BF16 = jnp.bfloat16


def rms_norm(tensor):
    floats = tensor.astype(F32)
    return (floats * lax.rsqrt(jnp.mean(floats * floats, axis=-1, keepdims=True) + EPSILON)).astype(BF16)


def dot(a, b):
    return jnp.dot(a, b, preferred_element_type=F32)


def dot_t(a, b):
    return lax.dot_general(a, b, (((1,), (1,)), ((), ())), preferred_element_type=F32)


def vmem():
    return pl.BlockSpec(memory_space=pltpu.VMEM)


def hbm():
    return pl.BlockSpec(memory_space=pltpu.HBM)


def params(mib):
    return pltpu.CompilerParams(vmem_limit_bytes=mib << 20)


def head_sides(width):
    lane = lax.broadcasted_iota(jnp.int32, (1, LANES), 1)
    return [(lane >= at) & (lane < at + width) for at in range(0, LANES, width)]


def softmax_part(query, keys, values, sides, bias=None, masks=None):
    peak = mixed = total = None
    for side in sides:
        if bias is None:
            score = dot_t(query, jnp.where(side, keys, jnp.zeros_like(keys)))
        else:
            score = dot_t(jnp.where(side, query, jnp.ones_like(query)), jnp.where(side, keys, bias))
        if masks:
            blocks = []
            for row in range(0, score.shape[0], ROWS):
                line = [score[row : row + ROWS, at : at + ROWS] for at in range(0, score.shape[1], ROWS)]
                for index, part in enumerate(line):
                    mask = masks.get((row // ROWS, index))
                    if mask is not None:
                        line[index] = part + mask
                blocks.append(jnp.concatenate(line, axis=1))
            score = jnp.concatenate(blocks, axis=0)
        top = jnp.max(score, axis=1, keepdims=True)
        weight = jnp.exp(score - top).astype(BF16)
        both = dot(weight, jnp.where(side, values, jnp.ones_like(values)))
        other = pltpu.roll(both, LANES // len(sides), 1)
        top = jnp.broadcast_to(top, both.shape)
        if peak is None:
            peak, mixed, total = top, both, other
        else:
            peak, mixed, total = (
                jnp.where(side, new, old) for new, old in ((top, peak), (both, mixed), (other, total))
            )
    return peak, mixed, total


def merge(first, second):
    peak = jnp.maximum(first[0], second[0])
    left, right = jnp.exp(first[0] - peak), jnp.exp(second[0] - peak)
    mixed = first[1] * left + second[1] * right
    total = first[2] * left + second[2] * right
    return mixed / total


def tile_at(tile):
    return pl.ds(pl.multiple_of(tile * LANES, LANES), LANES)


def row_step(nodes, keys):
    return nodes if nodes * keys <= SCORES else math.gcd(nodes, ROWS)


def project_observations(chunks, w_kv, keys, values, bias):
    feat = w_kv.shape[0]
    base = 0
    for chunk in chunks:
        size = chunk.shape[0]
        block = chunk[...].astype(F32)
        live = block[:, :1] < jnp.inf
        normed = rms_norm(jnp.where(live, block, 0.0))
        part = slice(base, base + size)
        keys[part] = dot(normed, w_kv[:, :feat]).astype(BF16)
        values[part] = dot(normed, w_kv[:, feat:]).astype(BF16)
        bias[part] = jnp.broadcast_to(jnp.where(live, 0.0, MASKED), (size, LANES)).astype(BF16)
        base += size


def cross_head_kernel(width, query, w_kv, *refs):
    chunks, (peak, mixed, total, keys, values, bias) = refs[:-6], refs[-6:]
    nodes, feat = query.shape
    project_observations(chunks, w_kv, keys, values, bias)
    sides = head_sides(width)
    step = row_step(nodes, keys.shape[0])

    @pl.loop(0, feat // LANES)
    def _(tile):
        at = tile_at(tile)
        for start in range(0, nodes, step):
            part = slice(start, start + step)
            peak[part, at], mixed[part, at], total[part, at] = softmax_part(
                query[part, at], keys[:, at], values[:, at], sides, bias[...]
            )


def cross_tail_kernel(
    width, latent, query, w_kv, w_out, peak, mixed, total, chunk, out, first, last, keys, values, bias, ctx
):
    nodes, feat = query.shape
    project_observations([chunk], w_kv, keys, values, bias)
    sides = head_sides(width)
    step = row_step(nodes, keys.shape[0])

    @pl.loop(0, feat // LANES)
    def _(tile):
        at = tile_at(tile)
        for start in range(0, nodes, step):
            part = slice(start, start + step)
            rest = softmax_part(query[part, at], keys[:, at], values[:, at], sides, bias[...])
            ctx[part, at] = merge((peak[part, at], mixed[part, at], total[part, at]), rest).astype(BF16)

    after = (latent[...].astype(F32) + dot(ctx[...], w_out[...])).astype(BF16)
    out[...] = after
    first[...] = after[: first.shape[0]]
    last[...] = after[nodes - last.shape[0] :]


def cross_attention(latent, queries, rows, w_kv, w_out, half):
    nodes, feat = latent.shape
    width = feat // HEADS
    chunks, last = rows[:-1], rows[-1]
    size = sum(chunk.shape[0] for chunk in chunks)
    state = pl.pallas_call(
        functools.partial(cross_head_kernel, width),
        out_shape=[jax.ShapeDtypeStruct((nodes, feat), F32)] * 3,
        in_specs=[vmem()] * (2 + len(chunks)),
        out_specs=[vmem()] * 3,
        scratch_shapes=[
            pltpu.VMEM((size, feat), BF16),
            pltpu.VMEM((size, feat), BF16),
            pltpu.VMEM((size, LANES), BF16),
        ],
        compiler_params=params(min(60, 14 + 16 * size // 1024)),
        cost_estimate=pl.CostEstimate(flops=16_000_000_000, bytes_accessed=12 << 20, transcendentals=0),
        name="cross_head",
    )(queries, w_kv, *chunks)
    size = last.shape[0]
    return pl.pallas_call(
        functools.partial(cross_tail_kernel, width),
        out_shape=[jax.ShapeDtypeStruct((count, feat), BF16) for count in (nodes, half, half)],
        in_specs=[vmem()] * 8,
        out_specs=[vmem()] * 3,
        scratch_shapes=[
            pltpu.VMEM((size, feat), BF16),
            pltpu.VMEM((size, feat), BF16),
            pltpu.VMEM((size, LANES), BF16),
            pltpu.VMEM((nodes, feat), BF16),
        ],
        compiler_params=params(20),
        cost_estimate=pl.CostEstimate(flops=7_000_000_000, bytes_accessed=12 << 20, transcendentals=0),
        name="cross_tail",
    )(latent, queries, w_kv, w_out, *state, last)


def edge_masks():
    row = lax.broadcasted_iota(jnp.int32, (ROWS, ROWS), 0)
    col = lax.broadcasted_iota(jnp.int32, (ROWS, ROWS), 1)
    return jnp.where(col >= row, 0.0, MASKED), jnp.where(col <= row, 0.0, MASKED)


def window_local_kernel(width, half, own, w_qkv, query, peak, mixed, total, keys, values):
    nodes, feat = own.shape
    normed = rms_norm(own[...])
    scale = jnp.asarray(1.0 / math.sqrt(width), BF16)
    query[...] = dot(normed, w_qkv[:, :feat]).astype(BF16) * scale
    keys[...] = dot(normed, w_qkv[:, feat : 2 * feat]).astype(BF16)
    values[...] = dot(normed, w_qkv[:, 2 * feat :]).astype(BF16)
    sides = head_sides(width)
    reach = half // ROWS
    count = nodes // ROWS
    before, after = edge_masks()

    masks = {}
    for block in range(count):
        for other in range(count):
            if other - block == -reach:
                masks[block, other] = before
            elif other - block == reach:
                masks[block, other] = after
            elif abs(other - block) > reach:
                masks[block, other] = MASKED

    @pl.loop(0, feat // LANES)
    def _(tile):
        at = tile_at(tile)
        peak[:, at], mixed[:, at], total[:, at] = softmax_part(
            query[:, at], keys[:, at], values[:, at], sides, masks=masks
        )


def window_halo_kernel(
    width, edge, own, query, peak, mixed, total, low, high, w_qkv, w_out, out, keys, values, bias, ctx
):
    nodes, feat = own.shape
    half = low.shape[0]
    for base, rows, gate in ((0, low, 0), (half, high, 1)):
        normed = rms_norm(rows[...])
        part = slice(base, base + half)
        keys[part] = dot(normed, w_qkv[:, feat : 2 * feat]).astype(BF16)
        values[part] = dot(normed, w_qkv[:, 2 * feat :]).astype(BF16)
        bias[part] = jnp.full((half, LANES), edge[gate], F32).astype(BF16)
    sides = head_sides(width)
    reach = half // ROWS
    count = nodes // ROWS
    before, after = edge_masks()

    @pl.loop(0, feat // LANES)
    def _(tile):
        at = tile_at(tile)
        for block in range(count):
            part = slice(block * ROWS, (block + 1) * ROWS)
            first, stop = min(block, reach), max(reach, block + 2 * reach - count + 1)
            state = (peak[part, at], mixed[part, at], total[part, at])
            if stop > first:
                masks = {}
                if block < reach:
                    masks[0, 0] = before
                if block + 2 * reach - count >= reach:
                    masks[0, stop - first - 1] = after
                span = slice(first * ROWS, stop * ROWS)
                other = softmax_part(query[part, at], keys[span, at], values[span, at], sides, bias[span], masks)
                ctx[part, at] = merge(state, other).astype(BF16)
            else:
                ctx[part, at] = (state[1] / state[2]).astype(BF16)

    out[...] = (own[...].astype(F32) + dot(ctx[...], w_out[...])).astype(BF16)


def window_local(own, half, w_qkv):
    nodes, feat = own.shape
    return pl.pallas_call(
        functools.partial(window_local_kernel, feat // HEADS, half),
        out_shape=[jax.ShapeDtypeStruct((nodes, feat), BF16)] + [jax.ShapeDtypeStruct((nodes, feat), F32)] * 3,
        in_specs=[vmem()] * 2,
        out_specs=[vmem()] * 4,
        scratch_shapes=[pltpu.VMEM((nodes, feat), BF16), pltpu.VMEM((nodes, feat), BF16)],
        compiler_params=params(24),
        cost_estimate=pl.CostEstimate(flops=15_000_000_000, bytes_accessed=12 << 20, transcendentals=0),
        name="window_local",
    )(own, w_qkv)


def window_halo(edge, own, local, low, high, w_qkv, w_out):
    nodes, feat = own.shape
    half = low.shape[0]
    return pl.pallas_call(
        functools.partial(window_halo_kernel, feat // HEADS),
        out_shape=jax.ShapeDtypeStruct((nodes, feat), BF16),
        in_specs=[pl.BlockSpec(memory_space=pltpu.SMEM)] + [vmem()] * 9,
        out_specs=vmem(),
        scratch_shapes=[
            pltpu.VMEM((2 * half, feat), BF16),
            pltpu.VMEM((2 * half, feat), BF16),
            pltpu.VMEM((2 * half, LANES), BF16),
            pltpu.VMEM((nodes, feat), BF16),
        ],
        compiler_params=params(24),
        cost_estimate=pl.CostEstimate(flops=10_000_000_000, bytes_accessed=12 << 20, transcendentals=0),
        name="window_halo",
    )(edge, own, *local, low, high, w_qkv, w_out)


def mlp_kernel(group, rows, *refs):
    pieces, (out, held, normed, total, sems) = refs[:-5], refs[-5:]
    slots = held.shape[0]
    blocks = [[]]
    filled = 0
    for piece in pieces:
        at = 0
        while at < piece.shape[0]:
            size = min(group - filled, piece.shape[0] - at)
            blocks[-1].append((piece, at, size, filled))
            at, filled = at + size, filled + size
            if filled == group:
                blocks.append([])
                filled = 0
    blocks.pop()

    def copies(index):
        slot = index % slots
        return [
            pltpu.make_async_copy(
                piece.at[pl.ds(at, size)], held.at[slot, pl.ds(filled, size)], sems.at[slot, filled]
            )
            for piece, at, size, filled in blocks[index]
        ]

    for index in range(min(slots, len(blocks))):
        for copy in copies(index):
            copy.start()
    normed[...] = rms_norm(rows[...])
    total[...] = rows[...].astype(F32)
    hidden = None
    for index in range(len(blocks) + 1):
        ready = None
        if index < len(blocks):
            for copy in copies(index):
                copy.wait()
            slot = index % slots
            ready = dot(normed[...], jnp.concatenate([held[slot, k, 0] for k in range(group)], axis=1))
        if index > 0:
            slot = (index - 1) % slots
            total[...] += dot_t(hidden, jnp.concatenate([held[slot, k, 1] for k in range(group)], axis=1))
            if index - 1 + slots < len(blocks):
                for copy in copies(index - 1 + slots):
                    copy.start()
        if ready is not None:
            hidden = jax.nn.gelu(ready, approximate=True).astype(BF16)
    out[...] = total[...].astype(BF16)


def mlp(rows, pieces):
    nodes, feat = rows.shape
    width = pieces[0].shape[-1]
    group = math.gcd(sum(piece.shape[0] for piece in pieces), max(1, 512 // width))
    return pl.pallas_call(
        functools.partial(mlp_kernel, group),
        out_shape=jax.ShapeDtypeStruct((nodes, feat), BF16),
        in_specs=[vmem()] + [hbm()] * len(pieces),
        out_specs=vmem(),
        scratch_shapes=[
            pltpu.VMEM((3, group, 2, feat, width), BF16),
            pltpu.VMEM((nodes, feat), BF16),
            pltpu.VMEM((nodes, feat), F32),
            pltpu.SemaphoreType.DMA((3, group)),
        ],
        compiler_params=params(18 + (12 * group * feat * max(width, LANES) >> 20)),
        cost_estimate=pl.CostEstimate(flops=8_000_000_000, bytes_accessed=18 << 20, transcendentals=0),
        name="mlp",
    )(rows, *pieces)


def shards(
    latent,
    observations,
    counts,
    cross_query,
    cross_kv,
    cross_out,
    self_qkv,
    self_out,
    mlp_in,
    mlp_out,
):
    everyone = ("loc", "stream")
    feat = latent.shape[1]
    width = feat // HEADS
    half = WIN // 2
    streams, places = lax.axis_size("stream"), lax.axis_size("loc")
    stream = lax.axis_index("stream")

    def rotate(value, shift):
        return lax.ppermute(value, "stream", [(i, (i + shift) % streams) for i in range(streams)])

    def pass_on(value, step):
        pairs = [(i, i + step) for i in range(1, streams - 1)]
        return lax.ppermute(value, "stream", pairs)

    def near_far(value):
        near = [rotate(value, shift) for shift in sorted({1, streams - 1} - {streams})]
        if streams == 4:
            far = [jnp.where(stream >= 2, pass_on(near[0], 1), pass_on(near[1], -1))]
        else:
            far = [rotate(value, shift) for shift in range(2, streams - 1)]
        return near, far

    def spread(piece):
        if places & (places - 1):
            return [lax.all_gather(piece, "loc", axis=0, tiled=True)]
        flip = [[(i, i ^ mask) for i in range(places)] for mask in range(places)]
        parts = [piece] + [lax.ppermute(piece, "loc", flip[mask]) for mask in range(2, places, 2)]
        return parts + [lax.ppermute(part, "loc", flip[1]) for part in parts]

    held = jnp.stack([mlp_in, mlp_out])[None]
    near, far = near_far(held)
    pieces = spread(held)
    if near:
        pieces += spread(jnp.concatenate(near))
    if far:
        pieces += spread(jnp.concatenate(far))
    slot = lax.broadcasted_iota(jnp.int32, observations.shape[:4], 3)
    marked = jnp.where((slot < counts[..., None])[..., None], observations, jnp.asarray(jnp.inf, BF16))
    moved = lax.all_to_all(marked, "loc", split_axis=2, concat_axis=1, tiled=True).reshape(-1, feat)
    near, far = near_far(moved)
    rows = [moved] + near + far
    queries = dot(rms_norm(latent), cross_query).astype(BF16) * jnp.asarray(1.0 / math.sqrt(width), BF16)
    after_cross, first, last = cross_attention(latent, queries, rows, cross_kv, cross_out, half)
    count = lax.axis_size(everyone)
    low = lax.ppermute(last, everyone, [(i, i + 1) for i in range(count - 1)])
    high = lax.ppermute(first, everyone, [(i + 1, i) for i in range(count - 1)])
    local = window_local(after_cross, half, self_qkv)
    place = lax.axis_index(everyone)
    edge = jnp.where(jnp.stack([place == 0, place == count - 1]), MASKED, 0.0).astype(F32)
    after_self = window_halo(edge, after_cross, local, low, high, self_qkv, self_out)
    return mlp(after_self, pieces)


def solution(mesh):
    return jax.shard_map(
        shards,
        mesh=mesh,
        in_specs=(
            P(("loc", "stream"), None),
            P("stream", "loc", None, None, None),
            P("stream", "loc", None),
            P(),
            P(),
            P(),
            P(),
            P(),
            P(None, ("loc", "stream")),
            P(None, ("loc", "stream")),
        ),
        out_specs=P(("loc", "stream"), None),
        check_vma=False,
    )
```

profile of v0, /device:TPU:0, one launch (start us, length us, event | category | flops | bytes accessed | tf_op | source)
XLA Modules:
  0.0 192.5 jit_solution(5596085634641291885)
XLA Ops:
  1.2 3.1 %collective-permute-start.13 = (bf16[1,2,1024,128]{3,2,1,0:T(8,128)(2,1)S(1)}, bf16[1,2,1024,128]{3,2,1,0:T(8,128)(2,1)}, u32[]{:S(2)}, u32[]{:S(2)}) collective-permute-start(bf16[1,2,1024,128]{3,2,1,0:T(8,128)(2,1)S(1)} %maximum_bitcast_fusion.refs_0_), channel_id=1, source_target_pairs={{0,1},{1,2},{2,3},{3,0},{4,5},{5,6},{6,7},{7,4},{8,9},{9,10},{10,1... | collective-permute-start | bytes 1572872 | tf_op jit(solution)/shard_map/ppermute | solution.py:392
  4.3 2.1 %collective-permute-start.14 = (bf16[1,2,1024,128]{3,2,1,0:T(8,128)(2,1)S(1)}, bf16[1,2,1024,128]{3,2,1,0:T(8,128)(2,1)}, u32[]{:S(2)}, u32[]{:S(2)}) collective-permute-start(bf16[1,2,1024,128]{3,2,1,0:T(8,128)(2,1)S(1)} %maximum_bitcast_fusion.refs_0_), channel_id=1, source_target_pairs={{0,3},{1,0},{2,1},{3,2},{4,7},{5,4},{6,5},{7,6},{8,11},{9,8},{10,9... | collective-permute-start | bytes 1572872 | tf_op jit(solution)/shard_map/ppermute | solution.py:392
  8.8 2.0 %bitcast_select_fusion = bf16[1,1,8,32,1024]{4,3,1,0,2:T(8,128)(2,1)} fusion(bf16[1,1,8,32,1024]{4,3,2,1,0:T(8,128)(2,1)} %param.11, pred[8,32]{1,0:T(8,128)(4,1)S(1)} %iota_compare_fusion), kind=kLoop, calls=%fused_computation.8 | loop fusion | flops 262144 | bytes 1048832 | tf_op jit(solution)/shard_map/jit(_where)/select_n | solution.py:421
  10.8 4.1 %all-to-all-start = ((bf16[1,1,8,32,1024]{4,3,1,0,2:T(8,128)(2,1)}), bf16[1,1,8,32,1024]{4,3,1,0,2:T(8,128)(2,1)}, u32[]{:S(2)}, u32[]{:S(2)}) async-start(bf16[1,1,8,32,1024]{4,3,1,0,2:T(8,128)(2,1)} %bitcast_select_fusion), calls=%async_computation | async-start | bytes 1048576 | tf_op jit(solution)/shard_map/all_to_all | solution.py:422
  16.8 9.8 %all-to-all-done = bf16[1,1,8,32,1024]{4,3,1,0,2:T(8,128)(2,1)} async-done(((bf16[1,1,8,32,1024]{4,3,1,0,2:T(8,128)(2,1)}), bf16[1,1,8,32,1024]{4,3,1,0,2:T(8,128)(2,1)}, u32[]{:S(2)}, u32[]{:S(2)}) %all-to-all-start) | async-done | bytes 524320 | tf_op jit(solution)/shard_map/all_to_all | solution.py:422
  26.7 4.0 %collective-permute-start.1 = (bf16[256,1024]{1,0:T(8,128)(2,1)}, bf16[256,1024]{1,0:T(8,128)(2,1)}, u32[]{:S(2)}, u32[]{:S(2)}) collective-permute-start(bf16[256,1024]{1,0:T(8,128)(2,1)} %bitcast.4.refs_0_), channel_id=1, source_target_pairs={{0,3},{1,0},{2,1},{3,2},{4,7},{5,4},{6,5},{7,6},{8,11},{9,8},{10,9... | collective-permute-start | bytes 1572872 | tf_op jit(solution)/shard_map/ppermute | solution.py:392
  36.4 7.2 %collective-permute-done.refs_1_ = bf16[256,1024]{1,0:T(8,128)(2,1)} collective-permute-done((bf16[256,1024]{1,0:T(8,128)(2,1)}, bf16[256,1024]{1,0:T(8,128)(2,1)}, u32[]{:S(2)}, u32[]{:S(2)}) %collective-permute-start) | collective-permute-done | bytes 524320 | tf_op jit(solution)/shard_map/ppermute | solution.py:392
  43.6 8.8 %collective-permute-done.1.refs_2_ = bf16[256,1024]{1,0:T(8,128)(2,1)} collective-permute-done((bf16[256,1024]{1,0:T(8,128)(2,1)}, bf16[256,1024]{1,0:T(8,128)(2,1)}, u32[]{:S(2)}, u32[]{:S(2)}) %collective-permute-start.1) | collective-permute-done | bytes 524320 | tf_op jit(solution)/shard_map/ppermute | solution.py:392
  53.8 8.9 %collective-permute-done.23 = bf16[1,2,1024,128]{3,2,1,0:T(8,128)(2,1)} collective-permute-done((bf16[1,2,1024,128]{3,2,1,0:T(8,128)(2,1)}, bf16[1,2,1024,128]{3,2,1,0:T(8,128)(2,1)}, u32[]{:S(2)}, u32[]{:S(2)}) %collective-permute-start.23) | collective-permute-done | bytes 524320 | tf_op jit(solution)/shard_map/ppermute | solution.py:396
  67.9 2.0 %constant_dynamic-update-slice_fusion.refs_8_ = bf16[2,2,1024,128]{3,2,1,0:T(8,128)(2,1)} fusion(bf16[2,2,1024,128]{3,2,1,0:T(8,128)(2,1)} %constant_dynamic-update-slice_fusion.1, bf16[1,2,1024,128]{3,2,1,0:T(8,128)(2,1)} %collective-permute-done.14), kind=kLoop, calls=%fused_computation.11 | loop fusion | bytes 1048576 | tf_op jit(solution)/shard_map/concatenate | solution.py:417
  74.5 6.0 %collective-permute-done.3 = bf16[256,1024]{1,0:T(8,128)(2,1)} collective-permute-done((bf16[256,1024]{1,0:T(8,128)(2,1)}, bf16[256,1024]{1,0:T(8,128)(2,1)}, u32[]{:S(2)}, u32[]{:S(2)}) %collective-permute-start.3) | collective-permute-done | bytes 524320 | tf_op jit(solution)/shard_map/ppermute | solution.py:396
  80.5 3.0 %collective-permute-start.26 = (bf16[1,2,1024,128]{3,2,1,0:T(8,128)(2,1)S(1)}, bf16[1,2,1024,128]{3,2,1,0:T(8,128)(2,1)S(1)}, u32[]{:S(2)}, u32[]{:S(2)}) collective-permute-start(bf16[1,2,1024,128]{3,2,1,0:T(8,128)(2,1)S(1)} %broadcast_select_fusion.refs_16_), channel_id=1, source_target_pairs={{0,24},{4,28},{8,16},{12,20},{16,8},{20,12},{24,0},{28,4},{1,25},{... | collective-permute-start | bytes 1572872 | tf_op jit(solution)/shard_map/ppermute | solution.py:410
  83.5 2.2 %copy-done.5 = bf16[1024,2048]{1,0:T(8,128)(2,1)S(1)} copy-done((bf16[1024,2048]{1,0:T(8,128)(2,1)S(1)}, bf16[1024,2048]{1,0:T(8,128)(2,1)}, u32[]{:S(2)}) %copy-start.5) | copy-done | bytes 4194328
  85.7 15.6 %cross_head.1 = (f32[384,1024]{1,0:T(8,128)S(1)}, f32[384,1024]{1,0:T(8,128)S(1)}, f32[384,1024]{1,0:T(8,128)S(1)}) custom-call(bf16[384,1024]{1,0:T(8,128)(2,1)S(1)} %copy-done.24, bf16[1024,2048]{1,0:T(8,128)(2,1)S(1)} %copy-done.5, bf16[256,1024]{1,0:T(8,128)(2,1)} %bitcast.4.refs_0_, bf16[256,1024]{1,0:T(8,128)(2,1)} %collective-permute-done.refs_1_, ...), custom_call_target="tpu_custom_call" | custom-call | flops 16000000000 | bytes 12582912 | tf_op jit(solution)/shard_map/cross_head/pallas_call | solution.py:162
  103.1 2.9 %collective-permute-start.17 = (bf16[2,2,1024,128]{3,2,1,0:T(8,128)(2,1)}, bf16[2,2,1024,128]{3,2,1,0:T(8,128)(2,1)}, u32[]{:S(2)}, u32[]{:S(2)}) collective-permute-start(bf16[2,2,1024,128]{3,2,1,0:T(8,128)(2,1)} %constant_dynamic-update-slice_fusion.refs_8_), channel_id=1, source_target_pairs={{0,24},{4,28},{8,16},{12,20},{16,8},{20,12},{24,0},{28,4},{1,25},{... | collective-permute-start | bytes 3145736 | tf_op jit(solution)/shard_map/ppermute | solution.py:410
  106.6 8.6 %cross_tail.1 = (bf16[384,1024]{1,0:T(8,128)(2,1)S(1)}, bf16[256,1024]{1,0:T(8,128)(2,1)S(1)}, bf16[256,1024]{1,0:T(8,128)(2,1)}) custom-call(bf16[384,1024]{1,0:T(8,128)(2,1)S(1)} %copy-done.1, bf16[384,1024]{1,0:T(8,128)(2,1)S(1)} %copy-done.24, bf16[1024,2048]{1,0:T(8,128)(2,1)S(1)} %copy-done.6, bf16[1024,1024]{1,0:T(8,128)(2,1)S(1)} %copy-done.7, ...), custom_call_target="tpu_custom_call" | custom-call | flops 7000000000 | bytes 12582912 | tf_op jit(solution)/shard_map/cross_tail/pallas_call | solution.py:177
  117.7 3.7 %collective-permute-start.4 = (bf16[256,1024]{1,0:T(8,128)(2,1)}, bf16[256,1024]{1,0:T(8,128)(2,1)S(1)}, u32[]{:S(2)}, u32[]{:S(2)}) collective-permute-start(bf16[256,1024]{1,0:T(8,128)(2,1)} %get-tuple-element.23), channel_id=1, source_target_pairs={{0,1},{1,2},{2,3},{3,4},{4,5},{5,6},{6,7},{7,8},{8,9},{9,10},{10,1... | collective-permute-start | bytes 1572872 | tf_op jit(solution)/shard_map/ppermute | solution.py:428
  121.5 10.8 %collective-permute-done.15.refs_9_ = bf16[2,2,1024,128]{3,2,1,0:T(8,128)(2,1)} collective-permute-done((bf16[2,2,1024,128]{3,2,1,0:T(8,128)(2,1)}, bf16[2,2,1024,128]{3,2,1,0:T(8,128)(2,1)}, u32[]{:S(2)}, u32[]{:S(2)}) %collective-permute-start.15) | collective-permute-done | bytes 1048608 | tf_op jit(solution)/shard_map/ppermute | solution.py:410
  133.5 15.6 %collective-permute-done.16.refs_10_ = bf16[2,2,1024,128]{3,2,1,0:T(8,128)(2,1)} collective-permute-done((bf16[2,2,1024,128]{3,2,1,0:T(8,128)(2,1)}, bf16[2,2,1024,128]{3,2,1,0:T(8,128)(2,1)}, u32[]{:S(2)}, u32[]{:S(2)}) %collective-permute-start.16) | collective-permute-done | bytes 1048608 | tf_op jit(solution)/shard_map/ppermute | solution.py:410
  149.1 3.4 %collective-permute-done.17.refs_11_ = bf16[2,2,1024,128]{3,2,1,0:T(8,128)(2,1)} collective-permute-done((bf16[2,2,1024,128]{3,2,1,0:T(8,128)(2,1)}, bf16[2,2,1024,128]{3,2,1,0:T(8,128)(2,1)}, u32[]{:S(2)}, u32[]{:S(2)}) %collective-permute-start.17) | collective-permute-done | bytes 1048608 | tf_op jit(solution)/shard_map/ppermute | solution.py:410
  153.9 2.8 %copy-done.4 = bf16[1024,3072]{1,0:T(8,128)(2,1)S(1)} copy-done((bf16[1024,3072]{1,0:T(8,128)(2,1)S(1)}, bf16[1024,3072]{1,0:T(8,128)(2,1)}, u32[]{:S(2)}) %copy-start.4) | copy-done | bytes 6291480
  157.9 10.0 %window_local.1 = (bf16[384,1024]{1,0:T(8,128)(2,1)S(1)}, f32[384,1024]{1,0:T(8,128)S(1)}, f32[384,1024]{1,0:T(8,128)S(1)}, f32[384,1024]{1,0:T(8,128)S(1)}) custom-call(bf16[384,1024]{1,0:T(8,128)(2,1)S(1)} %copy-done.26, bf16[1024,3072]{1,0:T(8,128)(2,1)S(1)} %copy-done.4), custom_call_target="tpu_custom_call" | custom-call | flops 15000000512 | bytes 12582912 | tf_op jit(solution)/shard_map/window_local/pallas_call | solution.py:270
  168.7 10.9 %window_halo.1.rows = bf16[384,1024]{1,0:T(8,128)(2,1)S(1)} custom-call(f32[2]{0:T(128)S(1)} %add_select_fusion.edge, bf16[384,1024]{1,0:T(8,128)(2,1)S(1)} %copy-done.27, bf16[384,1024]{1,0:T(8,128)(2,1)S(1)} %get-tuple-element.19.query, f32[384,1024]{1,0:T(8,128)S(1)} %get-tuple-element.20.peak, f32[384,1024]{1,0:T(8,128)S(1)} %get-tuple-element.21.mixed, ...), custom_call_target="tpu_custom_call" | custom-call | flops 10000000000 | bytes 12582912 | tf_op jit(solution)/shard_map/window_halo/pallas_call | solution.py:285
  179.6 12.7 %mlp.1 = bf16[384,1024]{1,0:T(8,128)(2,1)} custom-call(bf16[384,1024]{1,0:T(8,128)(2,1)S(1)} %window_halo.1.rows, bf16[1,2,1024,128]{3,2,1,0:T(8,128)(2,1)S(1)} %maximum_bitcast_fusion.refs_0_, bf16[1,2,1024,128]{3,2,1,0:T(8,128)(2,1)} %collective-permute-done.6.refs_1_, bf16[1,2,1024,128]{3,2,1,0:T(8,128)(2,1)} %collective-permute-done.7.refs_2_, ...), custom_call_target="tpu_custom_call" | custom-call | flops 8000000000 | bytes 18874368 | tf_op jit(solution)/shard_map/mlp/pallas_call | solution.py:355
  (112 shorter events, 31.9 us)
Async XLA Ops:
  1.2 25.4 %collective-permute-start.13 = (bf16[1,2,1024,128]{3,2,1,0:T(8,128)(2,1)S(1)}, bf16[1,2,1024,128]{3,2,1,0:T(8,128)(2,1)}, u32[]{:S(2)}, u32[]{:S(2)}) collective-permute-start(bf16[1,2,1024,128]{3,2,1,0:T(8,128)(2,1)S(1)} %maximum_bitcast_fusion.refs_0_), channel_id=1, source_target_pairs={{0,1},{1,2},{2,3},{3,0},{4,5},{5,6},{6,7},{7,4},{8,9},{9,10},{10,1... | collective-permute-start | bytes 1572872 | tf_op jit(solution)/shard_map/ppermute | solution.py:392
  4.3 26.3 %collective-permute-start.14 = (bf16[1,2,1024,128]{3,2,1,0:T(8,128)(2,1)S(1)}, bf16[1,2,1024,128]{3,2,1,0:T(8,128)(2,1)}, u32[]{:S(2)}, u32[]{:S(2)}) collective-permute-start(bf16[1,2,1024,128]{3,2,1,0:T(8,128)(2,1)S(1)} %maximum_bitcast_fusion.refs_0_), channel_id=1, source_target_pairs={{0,3},{1,0},{2,1},{3,2},{4,7},{5,4},{6,5},{7,6},{8,11},{9,8},{10,9... | collective-permute-start | bytes 1572872 | tf_op jit(solution)/shard_map/ppermute | solution.py:392
  6.4 25.7 %collective-permute-start.6 = (bf16[1,2,1024,128]{3,2,1,0:T(8,128)(2,1)S(1)}, bf16[1,2,1024,128]{3,2,1,0:T(8,128)(2,1)}, u32[]{:S(2)}, u32[]{:S(2)}) collective-permute-start(bf16[1,2,1024,128]{3,2,1,0:T(8,128)(2,1)S(1)} %maximum_bitcast_fusion.refs_0_), channel_id=1, source_target_pairs={{0,8},{4,12},{8,0},{12,4},{16,24},{20,28},{24,16},{28,20},{1,9},{5... | collective-permute-start | bytes 1572872 | tf_op jit(solution)/shard_map/ppermute | solution.py:410
  14.9 20.0 %collective-permute-start.7 = (bf16[1,2,1024,128]{3,2,1,0:T(8,128)(2,1)S(1)}, bf16[1,2,1024,128]{3,2,1,0:T(8,128)(2,1)}, u32[]{:S(2)}, u32[]{:S(2)}) collective-permute-start(bf16[1,2,1024,128]{3,2,1,0:T(8,128)(2,1)S(1)} %maximum_bitcast_fusion.refs_0_), channel_id=1, source_target_pairs={{0,16},{4,20},{8,24},{12,28},{16,0},{20,4},{24,8},{28,12},{1,17},{... | collective-permute-start | bytes 1572872 | tf_op jit(solution)/shard_map/ppermute | solution.py:410
  26.7 25.7 %collective-permute-start.1 = (bf16[256,1024]{1,0:T(8,128)(2,1)}, bf16[256,1024]{1,0:T(8,128)(2,1)}, u32[]{:S(2)}, u32[]{:S(2)}) collective-permute-start(bf16[256,1024]{1,0:T(8,128)(2,1)} %bitcast.4.refs_0_), channel_id=1, source_target_pairs={{0,3},{1,0},{2,1},{3,2},{4,7},{5,4},{6,5},{7,6},{8,11},{9,8},{10,9... | collective-permute-start | bytes 1572872 | tf_op jit(solution)/shard_map/ppermute | solution.py:392
  30.7 21.7 %collective-permute-start.22 = (bf16[1,2,1024,128]{3,2,1,0:T(8,128)(2,1)}, bf16[1,2,1024,128]{3,2,1,0:T(8,128)(2,1)}, u32[]{:S(2)}, u32[]{:S(2)}) collective-permute-start(bf16[1,2,1024,128]{3,2,1,0:T(8,128)(2,1)} %collective-permute-done.13), channel_id=1, source_target_pairs={{1,2},{2,3},{5,6},{6,7},{9,10},{10,11},{13,14},{14,15},{17,18},{18... | collective-permute-start | bytes 1572872 | tf_op jit(solution)/shard_map/ppermute | solution.py:396
  32.2 30.6 %collective-permute-start.23 = (bf16[1,2,1024,128]{3,2,1,0:T(8,128)(2,1)}, bf16[1,2,1024,128]{3,2,1,0:T(8,128)(2,1)}, u32[]{:S(2)}, u32[]{:S(2)}) collective-permute-start(bf16[1,2,1024,128]{3,2,1,0:T(8,128)(2,1)} %collective-permute-done.14), channel_id=1, source_target_pairs={{1,0},{2,1},{5,4},{6,5},{9,8},{10,9},{13,12},{14,13},{17,16},{18,1... | collective-permute-start | bytes 1572872 | tf_op jit(solution)/shard_map/ppermute | solution.py:396
  35.0 36.0 %collective-permute-start.8 = (bf16[1,2,1024,128]{3,2,1,0:T(8,128)(2,1)S(1)}, bf16[1,2,1024,128]{3,2,1,0:T(8,128)(2,1)}, u32[]{:S(2)}, u32[]{:S(2)}) collective-permute-start(bf16[1,2,1024,128]{3,2,1,0:T(8,128)(2,1)S(1)} %maximum_bitcast_fusion.refs_0_), channel_id=1, source_target_pairs={{0,24},{4,28},{8,16},{12,20},{16,8},{20,12},{24,0},{28,4},{1,25},{... | collective-permute-start | bytes 1572872 | tf_op jit(solution)/shard_map/ppermute | solution.py:410
  43.6 27.5 %collective-permute-start.9 = (bf16[1,2,1024,128]{3,2,1,0:T(8,128)(2,1)S(1)}, bf16[1,2,1024,128]{3,2,1,0:T(8,128)(2,1)}, u32[]{:S(2)}, u32[]{:S(2)}) collective-permute-start(bf16[1,2,1024,128]{3,2,1,0:T(8,128)(2,1)S(1)} %maximum_bitcast_fusion.refs_0_), channel_id=1, source_target_pairs={{0,4},{4,0},{8,12},{12,8},{16,20},{20,16},{24,28},{28,24},{1,5},{5... | collective-permute-start | bytes 1572872 | tf_op jit(solution)/shard_map/ppermute | solution.py:411
  52.4 20.6 %collective-permute-start.2 = (bf16[256,1024]{1,0:T(8,128)(2,1)}, bf16[256,1024]{1,0:T(8,128)(2,1)}, u32[]{:S(2)}, u32[]{:S(2)}) collective-permute-start(bf16[256,1024]{1,0:T(8,128)(2,1)} %collective-permute-done.refs_1_), channel_id=1, source_target_pairs={{1,2},{2,3},{5,6},{6,7},{9,10},{10,11},{13,14},{14,15},{17,18},{18... | collective-permute-start | bytes 1572872 | tf_op jit(solution)/shard_map/ppermute | solution.py:396
  70.9 31.5 %collective-permute-start.11 = (bf16[1,2,1024,128]{3,2,1,0:T(8,128)(2,1)}, bf16[1,2,1024,128]{3,2,1,0:T(8,128)(2,1)S(1)}, u32[]{:S(2)}, u32[]{:S(2)}) collective-permute-start(bf16[1,2,1024,128]{3,2,1,0:T(8,128)(2,1)} %collective-permute-done.7.refs_2_), channel_id=1, source_target_pairs={{0,4},{4,0},{8,12},{12,8},{16,20},{20,16},{24,28},{28,24},{1,5},{5... | collective-permute-start | bytes 1572872 | tf_op jit(solution)/shard_map/ppermute | solution.py:411
  71.0 32.0 %collective-permute-start.12 = (bf16[1,2,1024,128]{3,2,1,0:T(8,128)(2,1)}, bf16[1,2,1024,128]{3,2,1,0:T(8,128)(2,1)S(1)}, u32[]{:S(2)}, u32[]{:S(2)}) collective-permute-start(bf16[1,2,1024,128]{3,2,1,0:T(8,128)(2,1)} %collective-permute-done.8.refs_3_), channel_id=1, source_target_pairs={{0,4},{4,0},{8,12},{12,8},{16,20},{20,16},{24,28},{28,24},{1,5},{5... | collective-permute-start | bytes 1572872 | tf_op jit(solution)/shard_map/ppermute | solution.py:411
  71.5 31.6 %collective-permute-start.24 = (bf16[1,2,1024,128]{3,2,1,0:T(8,128)(2,1)S(1)}, bf16[1,2,1024,128]{3,2,1,0:T(8,128)(2,1)S(1)}, u32[]{:S(2)}, u32[]{:S(2)}) collective-permute-start(bf16[1,2,1024,128]{3,2,1,0:T(8,128)(2,1)S(1)} %broadcast_select_fusion.refs_16_), channel_id=1, source_target_pairs={{0,8},{4,12},{8,0},{12,4},{16,24},{20,28},{24,16},{28,20},{1,9},{5... | collective-permute-start | bytes 1572872 | tf_op jit(solution)/shard_map/ppermute | solution.py:410
  73.0 33.0 %collective-permute-start.25 = (bf16[1,2,1024,128]{3,2,1,0:T(8,128)(2,1)S(1)}, bf16[1,2,1024,128]{3,2,1,0:T(8,128)(2,1)S(1)}, u32[]{:S(2)}, u32[]{:S(2)}) collective-permute-start(bf16[1,2,1024,128]{3,2,1,0:T(8,128)(2,1)S(1)} %broadcast_select_fusion.refs_16_), channel_id=1, source_target_pairs={{0,16},{4,20},{8,24},{12,28},{16,0},{20,4},{24,8},{28,12},{1,17},{... | collective-permute-start | bytes 1572872 | tf_op jit(solution)/shard_map/ppermute | solution.py:410
  80.5 25.5 %collective-permute-start.26 = (bf16[1,2,1024,128]{3,2,1,0:T(8,128)(2,1)S(1)}, bf16[1,2,1024,128]{3,2,1,0:T(8,128)(2,1)S(1)}, u32[]{:S(2)}, u32[]{:S(2)}) collective-permute-start(bf16[1,2,1024,128]{3,2,1,0:T(8,128)(2,1)S(1)} %broadcast_select_fusion.refs_16_), channel_id=1, source_target_pairs={{0,24},{4,28},{8,16},{12,20},{16,8},{20,12},{24,0},{28,4},{1,25},{... | collective-permute-start | bytes 1572872 | tf_op jit(solution)/shard_map/ppermute | solution.py:410
  102.5 29.8 %collective-permute-start.15 = (bf16[2,2,1024,128]{3,2,1,0:T(8,128)(2,1)}, bf16[2,2,1024,128]{3,2,1,0:T(8,128)(2,1)}, u32[]{:S(2)}, u32[]{:S(2)}) collective-permute-start(bf16[2,2,1024,128]{3,2,1,0:T(8,128)(2,1)} %constant_dynamic-update-slice_fusion.refs_8_), channel_id=1, source_target_pairs={{0,8},{4,12},{8,0},{12,4},{16,24},{20,28},{24,16},{28,20},{1,9},{5... | collective-permute-start | bytes 3145736 | tf_op jit(solution)/shard_map/ppermute | solution.py:410
  103.0 46.1 %collective-permute-start.16 = (bf16[2,2,1024,128]{3,2,1,0:T(8,128)(2,1)}, bf16[2,2,1024,128]{3,2,1,0:T(8,128)(2,1)}, u32[]{:S(2)}, u32[]{:S(2)}) collective-permute-start(bf16[2,2,1024,128]{3,2,1,0:T(8,128)(2,1)} %constant_dynamic-update-slice_fusion.refs_8_), channel_id=1, source_target_pairs={{0,16},{4,20},{8,24},{12,28},{16,0},{20,4},{24,8},{28,12},{1,17},{... | collective-permute-start | bytes 3145736 | tf_op jit(solution)/shard_map/ppermute | solution.py:410
  103.1 49.4 %collective-permute-start.17 = (bf16[2,2,1024,128]{3,2,1,0:T(8,128)(2,1)}, bf16[2,2,1024,128]{3,2,1,0:T(8,128)(2,1)}, u32[]{:S(2)}, u32[]{:S(2)}) collective-permute-start(bf16[2,2,1024,128]{3,2,1,0:T(8,128)(2,1)} %constant_dynamic-update-slice_fusion.refs_8_), channel_id=1, source_target_pairs={{0,24},{4,28},{8,16},{12,20},{16,8},{20,12},{24,0},{28,4},{1,25},{... | collective-permute-start | bytes 3145736 | tf_op jit(solution)/shard_map/ppermute | solution.py:410
  106.0 46.5 %collective-permute-start.18 = (bf16[2,2,1024,128]{3,2,1,0:T(8,128)(2,1)}, bf16[2,2,1024,128]{3,2,1,0:T(8,128)(2,1)}, u32[]{:S(2)}, u32[]{:S(2)}) collective-permute-start(bf16[2,2,1024,128]{3,2,1,0:T(8,128)(2,1)} %constant_dynamic-update-slice_fusion.refs_8_), channel_id=1, source_target_pairs={{0,4},{4,0},{8,12},{12,8},{16,20},{20,16},{24,28},{28,24},{1,5},{5... | collective-permute-start | bytes 3145736 | tf_op jit(solution)/shard_map/ppermute | solution.py:411
  117.7 35.3 %collective-permute-start.4 = (bf16[256,1024]{1,0:T(8,128)(2,1)}, bf16[256,1024]{1,0:T(8,128)(2,1)S(1)}, u32[]{:S(2)}, u32[]{:S(2)}) collective-permute-start(bf16[256,1024]{1,0:T(8,128)(2,1)} %get-tuple-element.23), channel_id=1, source_target_pairs={{0,1},{1,2},{2,3},{3,4},{4,5},{5,6},{6,7},{7,8},{8,9},{9,10},{10,1... | collective-permute-start | bytes 1572872 | tf_op jit(solution)/shard_map/ppermute | solution.py:428
  132.2 35.7 %collective-permute-start.5 = (bf16[256,1024]{1,0:T(8,128)(2,1)}, bf16[256,1024]{1,0:T(8,128)(2,1)S(1)}, u32[]{:S(2)}, u32[]{:S(2)}) collective-permute-start(bf16[256,1024]{1,0:T(8,128)(2,1)} %copy-done.23), channel_id=1, source_target_pairs={{1,0},{2,1},{3,2},{4,3},{5,4},{6,5},{7,6},{8,7},{9,8},{10,9},{11,1... | collective-permute-start | bytes 1572872 | tf_op jit(solution)/shard_map/ppermute | solution.py:429
  152.5 27.0 %collective-permute-start.19 = (bf16[2,2,1024,128]{3,2,1,0:T(8,128)(2,1)}, bf16[2,2,1024,128]{3,2,1,0:T(8,128)(2,1)S(1)}, u32[]{:S(2)}, u32[]{:S(2)}) collective-permute-start(bf16[2,2,1024,128]{3,2,1,0:T(8,128)(2,1)} %collective-permute-done.15.refs_9_), channel_id=1, source_target_pairs={{0,4},{4,0},{8,12},{12,8},{16,20},{20,16},{24,28},{28,24},{1,5},{5... | collective-permute-start | bytes 3145736 | tf_op jit(solution)/shard_map/ppermute | solution.py:411
  152.6 27.0 %collective-permute-start.20 = (bf16[2,2,1024,128]{3,2,1,0:T(8,128)(2,1)}, bf16[2,2,1024,128]{3,2,1,0:T(8,128)(2,1)S(1)}, u32[]{:S(2)}, u32[]{:S(2)}) collective-permute-start(bf16[2,2,1024,128]{3,2,1,0:T(8,128)(2,1)} %collective-permute-done.16.refs_10_), channel_id=1, source_target_pairs={{0,4},{4,0},{8,12},{12,8},{16,20},{20,16},{24,28},{28,24},{1,5},{5... | collective-permute-start | bytes 3145736 | tf_op jit(solution)/shard_map/ppermute | solution.py:411
  153.9 25.7 %collective-permute-start.21 = (bf16[2,2,1024,128]{3,2,1,0:T(8,128)(2,1)}, bf16[2,2,1024,128]{3,2,1,0:T(8,128)(2,1)S(1)}, u32[]{:S(2)}, u32[]{:S(2)}) collective-permute-start(bf16[2,2,1024,128]{3,2,1,0:T(8,128)(2,1)} %collective-permute-done.17.refs_11_), channel_id=1, source_target_pairs={{0,4},{4,0},{8,12},{12,8},{16,20},{20,16},{24,28},{28,24},{1,5},{5... | collective-permute-start | bytes 3145736 | tf_op jit(solution)/shard_map/ppermute | solution.py:411
  (36 other events, 484.4 us)
where the time goes:
time: 194 us; the launch traced here: 193 us
  waiting for transfers between devices  71.8 us (37%)
  Pallas kernels  57.8 us (30%)
  starting transfers between devices  40.6 us (21%)
  local copies, waits for them, and re-layouts  13.4 us (7%)
  other arithmetic  6.44 us (3%)
    ppermute x9, waiting for transfers between devices, spread(): lax.ppermute(piece, 'loc', flip[mask])  31.1 us
    ppermute x4, waiting for transfers between devices, rotate(): lax.ppermute(value, 'stream', [(i, (i + shift) % streams) for i in range(...  16 us
    pallas_call x1, Pallas kernels, cross_attention(): pl.pallas_call(functools.partial(cross_head_kernel, width), out_shape=[ja...  15.6 us
    ppermute x4, waiting for transfers between devices, pass_on(): return lax.ppermute(value, 'stream', pairs)  14.9 us
    ppermute x9, starting transfers between devices, spread(): lax.ppermute(piece, 'loc', flip[mask])  14.6 us
    pallas_call x1, Pallas kernels, mlp(): pl.pallas_call(functools.partial(mlp_kernel, group), out_shape=jax.ShapeD...  12.7 us
    unnamed x57, local copies, waits for them, and re-layouts  11.4 us
    pallas_call x1, Pallas kernels, window_halo(): pl.pallas_call(functools.partial(window_halo_kernel, feat // HEADS), out_...  10.9 us
  transfers between devices with their start and end apart: 32, of which 9 were waited for; matrix products, arithmetic and copies ran while one was open for 6% of the time, Pallas kernels for 23%

commit v1 on v0

--- a/solution.py
+++ b/solution.py
@@ -122,11 +122,13 @@
     sides = head_sides(width)
     step = row_step(nodes, keys.shape[0])
 
-    @pl.loop(0, feat // LANES)
+    @pl.loop(0, feat // LANES, unroll=4)
     def _(tile):
         at = tile_at(tile)
-        for start in range(0, nodes, step):
-            part = slice(start, start + step)
+
+        @pl.loop(0, nodes // step)
+        def _(block):
+            part = pl.ds(pl.multiple_of(block * step, step), step)
             peak[part, at], mixed[part, at], total[part, at] = softmax_part(
                 query[part, at], keys[:, at], values[:, at], sides, bias[...]
             )
@@ -140,11 +142,13 @@
     sides = head_sides(width)
     step = row_step(nodes, keys.shape[0])
 
-    @pl.loop(0, feat // LANES)
+    @pl.loop(0, feat // LANES, unroll=1)
     def _(tile):
         at = tile_at(tile)
-        for start in range(0, nodes, step):
-            part = slice(start, start + step)
+
+        @pl.loop(0, nodes // step)
+        def _(block):
+            part = pl.ds(pl.multiple_of(block * step, step), step)
             rest = softmax_part(query[part, at], keys[:, at], values[:, at], sides, bias[...])
             ctx[part, at] = merge((peak[part, at], mixed[part, at], total[part, at]), rest).astype(BF16)
 
@@ -219,7 +223,7 @@
             elif abs(other - block) > reach:
                 masks[block, other] = MASKED
 
-    @pl.loop(0, feat // LANES)
+    @pl.loop(0, feat // LANES, unroll=4)
     def _(tile):
         at = tile_at(tile)
         peak[:, at], mixed[:, at], total[:, at] = softmax_part(
@@ -243,7 +247,7 @@
     count = nodes // ROWS
     before, after = edge_masks()
 
-    @pl.loop(0, feat // LANES)
+    @pl.loop(0, feat // LANES, unroll=2)
     def _(tile):
         at = tile_at(tile)
         for block in range(count):
@@ -299,7 +303,12 @@
     )(edge, own, *local, low, high, w_qkv, w_out)
 
 
-def mlp_kernel(group, rows, *refs):
+def gelu(x):
+    slope = 2.0 * math.sqrt(2.0 / math.pi)
+    return x * jax.nn.sigmoid(x * (slope + slope * 0.044715 * (x * x)))
+
+
+def mlp_kernel(group, rows, base, *refs):
     pieces, (out, held, normed, total, sems) = refs[:-5], refs[-5:]
     slots = held.shape[0]
     blocks = [[]]
@@ -328,7 +337,7 @@
         for copy in copies(index):
             copy.start()
     normed[...] = rms_norm(rows[...])
-    total[...] = rows[...].astype(F32)
+    total[...] = base[...].astype(F32)
     hidden = None
     for index in range(len(blocks) + 1):
         ready = None
@@ -344,18 +353,18 @@
                 for copy in copies(index - 1 + slots):
                     copy.start()
         if ready is not None:
-            hidden = jax.nn.gelu(ready, approximate=True).astype(BF16)
-    out[...] = total[...].astype(BF16)
-
-
-def mlp(rows, pieces):
+            hidden = gelu(ready).astype(BF16)
+    out[...] = total[...].astype(out.dtype)
+
+
+def mlp(rows, base, pieces, dtype):
     nodes, feat = rows.shape
     width = pieces[0].shape[-1]
-    group = math.gcd(sum(piece.shape[0] for piece in pieces), max(1, 512 // width))
+    group = math.gcd(sum(piece.shape[0] for piece in pieces), max(1, 1024 // max(width, LANES)))
     return pl.pallas_call(
         functools.partial(mlp_kernel, group),
-        out_shape=jax.ShapeDtypeStruct((nodes, feat), BF16),
-        in_specs=[vmem()] + [hbm()] * len(pieces),
+        out_shape=jax.ShapeDtypeStruct((nodes, feat), dtype),
+        in_specs=[vmem()] * 2 + [hbm()] * len(pieces),
         out_specs=vmem(),
         scratch_shapes=[
             pltpu.VMEM((3, group, 2, feat, width), BF16),
@@ -364,9 +373,8 @@
             pltpu.SemaphoreType.DMA((3, group)),
         ],
         compiler_params=params(18 + (12 * group * feat * max(width, LANES) >> 20)),
-        cost_estimate=pl.CostEstimate(flops=8_000_000_000, bytes_accessed=18 << 20, transcendentals=0),
-        name="mlp",
-    )(rows, *pieces)
+        cost_estimate=pl.CostEstimate(flops=6_000_000_000, bytes_accessed=12 << 20, transcendentals=0),
+    )(rows, base, *pieces)
 
 
 def shards(
@@ -403,20 +411,25 @@
             far = [rotate(value, shift) for shift in range(2, streams - 1)]
         return near, far
 
-    def spread(piece):
+    def spread(piece, turn):
         if places & (places - 1):
             return [lax.all_gather(piece, "loc", axis=0, tiled=True)]
         flip = [[(i, i ^ mask) for i in range(places)] for mask in range(places)]
-        parts = [piece] + [lax.ppermute(piece, "loc", flip[mask]) for mask in range(2, places, 2)]
+        masks = [1 << bit for bit in range(1, places.bit_length() - 1)][::turn]
+        parts = [piece]
+        for mask in masks:
+            for part in list(parts):
+                parts.append(lax.ppermute(part, "loc", flip[mask]))
         return parts + [lax.ppermute(part, "loc", flip[1]) for part in parts]
 
     held = jnp.stack([mlp_in, mlp_out])[None]
     near, far = near_far(held)
-    pieces = spread(held)
-    if near:
-        pieces += spread(jnp.concatenate(near))
-    if far:
-        pieces += spread(jnp.concatenate(far))
+    pieces = spread(held, 1)
+    for index, piece in enumerate(near):
+        pieces += spread(piece, 1 - 2 * (index % 2))
+    late = []
+    for index, piece in enumerate(far):
+        late += spread(piece, 2 * (index % 2) - 1)
     slot = lax.broadcasted_iota(jnp.int32, observations.shape[:4], 3)
     marked = jnp.where((slot < counts[..., None])[..., None], observations, jnp.asarray(jnp.inf, BF16))
     moved = lax.all_to_all(marked, "loc", split_axis=2, concat_axis=1, tiled=True).reshape(-1, feat)
@@ -431,7 +444,10 @@
     place = lax.axis_index(everyone)
     edge = jnp.where(jnp.stack([place == 0, place == count - 1]), MASKED, 0.0).astype(F32)
     after_self = window_halo(edge, after_cross, local, low, high, self_qkv, self_out)
-    return mlp(after_self, pieces)
+    if not late:
+        return mlp(after_self, after_self, pieces, BF16)
+    partial = mlp(after_self, after_self, pieces, F32)
+    return mlp(after_self, partial, late, BF16)
 
 
 def solution(mesh):

time: 194 us -> 157 us (0.81)
  the two profiles are of different devices: /device:TPU:0 before, /device:TPU:25 now
where the time goes in v1:
time: 157 us
  starting transfers between devices  59.4 us (38%)
  Pallas kernels  49.1 us (31%)
  waiting for transfers between devices  42.5 us (27%)
  other arithmetic  4.34 us (3%)
    ppermute x16, starting transfers between devices, spread(): return parts + [lax.ppermute(part, 'loc', flip[1]) for part in parts]  18.8 us
    ppermute x4, waiting for transfers between devices, rotate(): lax.ppermute(value, 'stream', [(i, (i + shift) % streams) for i in range(...  18.8 us
    ppermute x12, starting transfers between devices, spread(): parts.append(lax.ppermute(part, 'loc', flip[mask]))  14.7 us
    pallas_call x1, Pallas kernels, cross_attention(): pl.pallas_call(functools.partial(cross_head_kernel, width), out_shape=[ja...  12.1 us
    ppermute x1, waiting for transfers between devices, shards(): high = lax.ppermute(first, everyone, [(i + 1, i) for i in range(count - 1)])  11.3 us
    pallas_call x2, Pallas kernels, mlp(): pl.pallas_call(functools.partial(mlp_kernel, group), out_shape=jax.ShapeD...  10.7 us
    pallas_call x1, Pallas kernels, window_halo(): pl.pallas_call(functools.partial(window_halo_kernel, feat // HEADS), out_...  9.65 us
    pallas_call x1, Pallas kernels, window_local(): pl.pallas_call(functools.partial(window_local_kernel, feat // HEADS, half...  9 us
  transfers between devices with their start and end apart: 39, of which 7 were waited for; matrix products, arithmetic and copies ran while one was open for 3% of the time, Pallas kernels for 29%

profile of v1, /device:TPU:25, one launch (start us, length us, event | category | flops | bytes accessed | tf_op | source)
XLA Modules:
  0.0 156.9 jit_solution(17683922868142812704)
XLA Ops:
  5.9 2.0 %bitcast_select_fusion = bf16[1,1,8,32,1024]{4,3,1,0,2:T(8,128)(2,1)} fusion(bf16[1,1,8,32,1024]{4,3,2,1,0:T(8,128)(2,1)} %param.11, pred[8,32]{1,0:T(8,128)(4,1)S(1)} %iota_compare_fusion), kind=kLoop, calls=%fused_computation.8 | loop fusion | flops 262144 | bytes 1048832 | tf_op jit(solution)/shard_map/jit(_where)/select_n | solution.py:434
  7.9 5.8 %all-to-all-start = ((bf16[1,1,8,32,1024]{4,3,1,0,2:T(8,128)(2,1)}), bf16[1,1,8,32,1024]{4,3,1,0,2:T(8,128)(2,1)}, u32[]{:S(2)}, u32[]{:S(2)}) async-start(bf16[1,1,8,32,1024]{4,3,1,0,2:T(8,128)(2,1)} %bitcast_select_fusion), calls=%async_computation | async-start | bytes 1048576 | tf_op jit(solution)/shard_map/all_to_all | solution.py:435
  14.2 7.3 %all-to-all-done = bf16[1,1,8,32,1024]{4,3,1,0,2:T(8,128)(2,1)} async-done(((bf16[1,1,8,32,1024]{4,3,1,0,2:T(8,128)(2,1)}), bf16[1,1,8,32,1024]{4,3,1,0,2:T(8,128)(2,1)}, u32[]{:S(2)}, u32[]{:S(2)}) %all-to-all-start) | async-done | bytes 524320 | tf_op jit(solution)/shard_map/all_to_all | solution.py:435
  21.5 1.9 %collective-permute-start = (bf16[256,1024]{1,0:T(8,128)(2,1)}, bf16[256,1024]{1,0:T(8,128)(2,1)S(1)}, u32[]{:S(2)}, u32[]{:S(2)}) collective-permute-start(bf16[256,1024]{1,0:T(8,128)(2,1)} %bitcast.4.refs_0_), channel_id=1, source_target_pairs={{0,1},{1,2},{2,3},{3,0},{4,5},{5,6},{6,7},{7,4},{8,9},{9,10},{10,1... | collective-permute-start | bytes 1572872 | tf_op jit(solution)/shard_map/ppermute | solution.py:400
  23.4 1.9 %collective-permute-done.21.refs_16_ = bf16[1,2,1024,128]{3,2,1,0:T(8,128)(2,1)} collective-permute-done((bf16[1,2,1024,128]{3,2,1,0:T(8,128)(2,1)S(1)}, bf16[1,2,1024,128]{3,2,1,0:T(8,128)(2,1)}, u32[]{:S(2)}, u32[]{:S(2)}) %collective-permute-start.21) | collective-permute-done | bytes 524320 | tf_op jit(solution)/shard_map/ppermute | solution.py:400
  29.4 5.2 %collective-permute-done.refs_1_ = bf16[256,1024]{1,0:T(8,128)(2,1)S(1)} collective-permute-done((bf16[256,1024]{1,0:T(8,128)(2,1)}, bf16[256,1024]{1,0:T(8,128)(2,1)S(1)}, u32[]{:S(2)}, u32[]{:S(2)}) %collective-permute-start) | collective-permute-done | bytes 524320 | tf_op jit(solution)/shard_map/ppermute | solution.py:400
  35.8 11.7 %collective-permute-done.1.refs_2_ = bf16[256,1024]{1,0:T(8,128)(2,1)S(1)} collective-permute-done((bf16[256,1024]{1,0:T(8,128)(2,1)}, bf16[256,1024]{1,0:T(8,128)(2,1)S(1)}, u32[]{:S(2)}, u32[]{:S(2)}) %collective-permute-start.1) | collective-permute-done | bytes 524320 | tf_op jit(solution)/shard_map/ppermute | solution.py:400
  50.5 12.1 %cross_head.1 = (f32[384,1024]{1,0:T(8,128)S(1)}, f32[384,1024]{1,0:T(8,128)S(1)}, f32[384,1024]{1,0:T(8,128)S(1)}) custom-call(bf16[384,1024]{1,0:T(8,128)(2,1)S(1)} %fusion.2.query, bf16[1024,2048]{1,0:T(8,128)(2,1)S(1)} %copy-done.2, bf16[256,1024]{1,0:T(8,128)(2,1)} %bitcast.4.refs_0_, bf16[256,1024]{1,0:T(8,128)(2,1)S(1)} %collective-permute-done.refs_1_, ...), custom_call_target="tpu_custom_call" | custom-call | flops 16000000000 | bytes 12582912 | tf_op jit(solution)/shard_map/cross_head/pallas_call | solution.py:166
  63.9 3.3 %collective-permute-start.17 = (bf16[1,2,1024,128]{3,2,1,0:T(8,128)(2,1)}, bf16[1,2,1024,128]{3,2,1,0:T(8,128)(2,1)S(1)}, u32[]{:S(2)}, u32[]{:S(2)}) collective-permute-start(bf16[1,2,1024,128]{3,2,1,0:T(8,128)(2,1)} %collective-permute-done.13.refs_8_), channel_id=1, source_target_pairs={{0,4},{4,0},{8,12},{12,8},{16,20},{20,16},{24,28},{28,24},{1,5},{5... | collective-permute-start | bytes 1572872 | tf_op jit(solution)/shard_map/ppermute | solution.py:423
  67.3 1.5 collective-permute-start.8
  68.9 4.6 %collective-permute-start.10 = (bf16[1,2,1024,128]{3,2,1,0:T(8,128)(2,1)}, bf16[1,2,1024,128]{3,2,1,0:T(8,128)(2,1)S(1)}, u32[]{:S(2)}, u32[]{:S(2)}) collective-permute-start(bf16[1,2,1024,128]{3,2,1,0:T(8,128)(2,1)} %collective-permute-done.6.refs_1_), channel_id=1, source_target_pairs={{0,4},{4,0},{8,12},{12,8},{16,20},{20,16},{24,28},{28,24},{1,5},{5... | collective-permute-start | bytes 1572872 | tf_op jit(solution)/shard_map/ppermute | solution.py:423
  73.6 3.6 %collective-permute-start.11 = (bf16[1,2,1024,128]{3,2,1,0:T(8,128)(2,1)}, bf16[1,2,1024,128]{3,2,1,0:T(8,128)(2,1)S(1)}, u32[]{:S(2)}, u32[]{:S(2)}) collective-permute-start(bf16[1,2,1024,128]{3,2,1,0:T(8,128)(2,1)} %collective-permute-done.7.refs_2_), channel_id=1, source_target_pairs={{0,4},{4,0},{8,12},{12,8},{16,20},{20,16},{24,28},{28,24},{1,5},{5... | collective-permute-start | bytes 1572872 | tf_op jit(solution)/shard_map/ppermute | solution.py:423
  80.2 3.6 %collective-permute-start.26 = (bf16[1,2,1024,128]{3,2,1,0:T(8,128)(2,1)S(1)}, bf16[1,2,1024,128]{3,2,1,0:T(8,128)(2,1)S(1)}, u32[]{:S(2)}, u32[]{:S(2)}) collective-permute-start(bf16[1,2,1024,128]{3,2,1,0:T(8,128)(2,1)S(1)} %collective-permute-done.22.refs_17_), channel_id=1, source_target_pairs={{0,4},{4,0},{8,12},{12,8},{16,20},{20,16},{24,28},{28,24},{1,5},{5... | collective-permute-start | bytes 1572872 | tf_op jit(solution)/shard_map/ppermute | solution.py:423
  83.8 7.7 %cross_tail.1 = (bf16[384,1024]{1,0:T(8,128)(2,1)S(1)}, bf16[256,1024]{1,0:T(8,128)(2,1)S(1)}, bf16[256,1024]{1,0:T(8,128)(2,1)S(1)}) custom-call(bf16[384,1024]{1,0:T(8,128)(2,1)S(1)} %copy-done.1, bf16[384,1024]{1,0:T(8,128)(2,1)S(1)} %fusion.2.query, bf16[1024,2048]{1,0:T(8,128)(2,1)S(1)} %copy-done.2, bf16[1024,1024]{1,0:T(8,128)(2,1)S(1)} %copy-done.3, ...), custom_call_target="tpu_custom_call" | custom-call | flops 7000000000 | bytes 12582912 | tf_op jit(solution)/shard_map/cross_tail/pallas_call | solution.py:181
  91.5 1.6 %collective-permute-start.31 = (bf16[1,2,1024,128]{3,2,1,0:T(8,128)(2,1)S(1)}, bf16[1,2,1024,128]{3,2,1,0:T(8,128)(2,1)S(1)}, u32[]{:S(2)}, u32[]{:S(2)}) collective-permute-start(bf16[1,2,1024,128]{3,2,1,0:T(8,128)(2,1)S(1)} %broadcast_select_fusion.refs_0_), channel_id=1, source_target_pairs={{0,16},{4,20},{8,24},{12,28},{16,0},{20,4},{24,8},{28,12},{1,17},{... | collective-permute-start | bytes 1572872 | tf_op jit(solution)/shard_map/ppermute | solution.py:422
  93.6 6.1 %collective-permute-start.4 = (bf16[256,1024]{1,0:T(8,128)(2,1)S(1)}, bf16[256,1024]{1,0:T(8,128)(2,1)S(1)}, u32[]{:S(2)}, u32[]{:S(2)}) collective-permute-start(bf16[256,1024]{1,0:T(8,128)(2,1)S(1)} %get-tuple-element.23), channel_id=1, source_target_pairs={{0,1},{1,2},{2,3},{3,4},{4,5},{5,6},{6,7},{7,8},{8,9},{9,10},{10,1... | collective-permute-start | bytes 1572872 | tf_op jit(solution)/shard_map/ppermute | solution.py:441
  99.7 5.9 %collective-permute-start.5 = (bf16[256,1024]{1,0:T(8,128)(2,1)S(1)}, bf16[256,1024]{1,0:T(8,128)(2,1)S(1)}, u32[]{:S(2)}, u32[]{:S(2)}) collective-permute-start(bf16[256,1024]{1,0:T(8,128)(2,1)S(1)} %get-tuple-element.24), channel_id=1, source_target_pairs={{1,0},{2,1},{3,2},{4,3},{5,4},{6,5},{7,6},{8,7},{9,8},{10,9},{11,1... | collective-permute-start | bytes 1572872 | tf_op jit(solution)/shard_map/ppermute | solution.py:442
  105.7 9.0 %window_local.1 = (bf16[384,1024]{1,0:T(8,128)(2,1)S(1)}, f32[384,1024]{1,0:T(8,128)S(1)}, f32[384,1024]{1,0:T(8,128)S(1)}, f32[384,1024]{1,0:T(8,128)S(1)}) custom-call(bf16[384,1024]{1,0:T(8,128)(2,1)S(1)} %get-tuple-element.18.own, bf16[1024,3072]{1,0:T(8,128)(2,1)S(1)} %bitcast.12), custom_call_target="tpu_custom_call" | custom-call | flops 15000000512 | bytes 12582912 | tf_op jit(solution)/shard_map/window_local/pallas_call | solution.py:274
  116.6 11.3 %collective-permute-done.5.high = bf16[256,1024]{1,0:T(8,128)(2,1)S(1)} collective-permute-done((bf16[256,1024]{1,0:T(8,128)(2,1)S(1)}, bf16[256,1024]{1,0:T(8,128)(2,1)S(1)}, u32[]{:S(2)}, u32[]{:S(2)}) %collective-permute-start.5) | collective-permute-done | bytes 524320 | tf_op jit(solution)/shard_map/ppermute | solution.py:442
  127.9 2.2 %collective-permute-start.33 = (bf16[1,2,1024,128]{3,2,1,0:T(8,128)(2,1)S(1)}, bf16[1,2,1024,128]{3,2,1,0:T(8,128)(2,1)S(1)}, u32[]{:S(2)}, u32[]{:S(2)}) collective-permute-start(bf16[1,2,1024,128]{3,2,1,0:T(8,128)(2,1)S(1)} %collective-permute-done.31.refs_1_), channel_id=1, source_target_pairs={{0,8},{4,12},{8,0},{12,4},{16,24},{20,28},{24,16},{28,20},{1,9},{5... | collective-permute-start | bytes 1572872 | tf_op jit(solution)/shard_map/ppermute | solution.py:422
  130.1 9.7 %window_halo.1.rows.base = bf16[384,1024]{1,0:T(8,128)(2,1)S(1)} custom-call(f32[2]{0:T(128)S(1)} %add_select_fusion.edge, bf16[384,1024]{1,0:T(8,128)(2,1)S(1)} %get-tuple-element.18.own, bf16[384,1024]{1,0:T(8,128)(2,1)S(1)} %get-tuple-element.19.query, f32[384,1024]{1,0:T(8,128)S(1)} %get-tuple-element.20.peak, f32[384,1024]{1,0:T(8,128)S(1)} %get-tuple-element.21.mixed, ...), custom_call_target="tpu_custom_call" | custom-call | flops 10000000000 | bytes 12582912 | tf_op jit(solution)/shard_map/window_halo/pallas_call | solution.py:289
  140.4 4.7 %collective-permute-done.33.refs_3_ = bf16[1,2,1024,128]{3,2,1,0:T(8,128)(2,1)S(1)} collective-permute-done((bf16[1,2,1024,128]{3,2,1,0:T(8,128)(2,1)S(1)}, bf16[1,2,1024,128]{3,2,1,0:T(8,128)(2,1)S(1)}, u32[]{:S(2)}, u32[]{:S(2)}) %collective-permute-start.33) | collective-permute-done | bytes 524320 | tf_op jit(solution)/shard_map/ppermute | solution.py:422
  145.9 7.2 %shard_map.100.base = f32[384,1024]{1,0:T(8,128)S(1)} custom-call(bf16[384,1024]{1,0:T(8,128)(2,1)S(1)} %window_halo.1.rows.base, bf16[384,1024]{1,0:T(8,128)(2,1)S(1)} %window_halo.1.rows.base, bf16[1,2,1024,128]{3,2,1,0:T(8,128)(2,1)S(1)} %maximum_bitcast_fusion.refs_0_, bf16[1,2,1024,128]{3,2,1,0:T(8,128)(2,1)} %collective-permute-done.6.refs_1_, ...), custom_call_target="tpu_custom_call" | custom-call | flops 6000000000 | bytes 12582912 | tf_op jit(solution)/shard_map/pallas_call | solution.py:364
  153.1 3.5 %shard_map.101 = bf16[384,1024]{1,0:T(8,128)(2,1)} custom-call(bf16[384,1024]{1,0:T(8,128)(2,1)S(1)} %window_halo.1.rows.base, f32[384,1024]{1,0:T(8,128)S(1)} %shard_map.100.base, bf16[1,2,1024,128]{3,2,1,0:T(8,128)(2,1)S(1)} %broadcast_select_fusion.refs_0_, bf16[1,2,1024,128]{3,2,1,0:T(8,128)(2,1)S(1)} %collective-permute-done.31.refs_1_, ...), custom_call_target="tpu_custom_call" | custom-call | flops 6000000000 | bytes 12582912 | tf_op jit(solution)/shard_map/pallas_call | solution.py:364
  (84 shorter events, 23.1 us)
Async XLA Ops:
  1.2 20.3 %collective-permute-start.13 = (bf16[1,2,1024,128]{3,2,1,0:T(8,128)(2,1)S(1)}, bf16[1,2,1024,128]{3,2,1,0:T(8,128)(2,1)}, u32[]{:S(2)}, u32[]{:S(2)}) collective-permute-start(bf16[1,2,1024,128]{3,2,1,0:T(8,128)(2,1)S(1)} %maximum_bitcast_fusion.refs_0_), channel_id=1, source_target_pairs={{0,1},{1,2},{2,3},{3,0},{4,5},{5,6},{6,7},{7,4},{8,9},{9,10},{10,1... | collective-permute-start | bytes 1572872 | tf_op jit(solution)/shard_map/ppermute | solution.py:400
  1.3 24.0 %collective-permute-start.21 = (bf16[1,2,1024,128]{3,2,1,0:T(8,128)(2,1)S(1)}, bf16[1,2,1024,128]{3,2,1,0:T(8,128)(2,1)}, u32[]{:S(2)}, u32[]{:S(2)}) collective-permute-start(bf16[1,2,1024,128]{3,2,1,0:T(8,128)(2,1)S(1)} %maximum_bitcast_fusion.refs_0_), channel_id=1, source_target_pairs={{0,3},{1,0},{2,1},{3,2},{4,7},{5,4},{6,5},{7,6},{8,11},{9,8},{10,9... | collective-permute-start | bytes 1572872 | tf_op jit(solution)/shard_map/ppermute | solution.py:400
  2.8 23.0 %collective-permute-start.6 = (bf16[1,2,1024,128]{3,2,1,0:T(8,128)(2,1)S(1)}, bf16[1,2,1024,128]{3,2,1,0:T(8,128)(2,1)}, u32[]{:S(2)}, u32[]{:S(2)}) collective-permute-start(bf16[1,2,1024,128]{3,2,1,0:T(8,128)(2,1)S(1)} %maximum_bitcast_fusion.refs_0_), channel_id=1, source_target_pairs={{0,8},{4,12},{8,0},{12,4},{16,24},{20,28},{24,16},{28,20},{1,9},{5... | collective-permute-start | bytes 1572872 | tf_op jit(solution)/shard_map/ppermute | solution.py:422
  4.0 22.8 %collective-permute-start.7 = (bf16[1,2,1024,128]{3,2,1,0:T(8,128)(2,1)S(1)}, bf16[1,2,1024,128]{3,2,1,0:T(8,128)(2,1)}, u32[]{:S(2)}, u32[]{:S(2)}) collective-permute-start(bf16[1,2,1024,128]{3,2,1,0:T(8,128)(2,1)S(1)} %maximum_bitcast_fusion.refs_0_), channel_id=1, source_target_pairs={{0,16},{4,20},{8,24},{12,28},{16,0},{20,4},{24,8},{28,12},{1,17},{... | collective-permute-start | bytes 1572872 | tf_op jit(solution)/shard_map/ppermute | solution.py:422
  25.3 22.3 %collective-permute-start.1 = (bf16[256,1024]{1,0:T(8,128)(2,1)}, bf16[256,1024]{1,0:T(8,128)(2,1)S(1)}, u32[]{:S(2)}, u32[]{:S(2)}) collective-permute-start(bf16[256,1024]{1,0:T(8,128)(2,1)} %bitcast.4.refs_0_), channel_id=1, source_target_pairs={{0,3},{1,0},{2,1},{3,2},{4,7},{5,4},{6,5},{7,6},{8,11},{9,8},{10,9... | collective-permute-start | bytes 1572872 | tf_op jit(solution)/shard_map/ppermute | solution.py:400
  25.8 22.5 %collective-permute-start.14 = (bf16[1,2,1024,128]{3,2,1,0:T(8,128)(2,1)}, bf16[1,2,1024,128]{3,2,1,0:T(8,128)(2,1)S(1)}, u32[]{:S(2)}, u32[]{:S(2)}) collective-permute-start(bf16[1,2,1024,128]{3,2,1,0:T(8,128)(2,1)} %collective-permute-done.13.refs_8_), channel_id=1, source_target_pairs={{0,8},{4,12},{8,0},{12,4},{16,24},{20,28},{24,16},{28,20},{1,9},{5... | collective-permute-start | bytes 1572872 | tf_op jit(solution)/shard_map/ppermute | solution.py:422
  26.8 22.8 %collective-permute-start.22 = (bf16[1,2,1024,128]{3,2,1,0:T(8,128)(2,1)}, bf16[1,2,1024,128]{3,2,1,0:T(8,128)(2,1)S(1)}, u32[]{:S(2)}, u32[]{:S(2)}) collective-permute-start(bf16[1,2,1024,128]{3,2,1,0:T(8,128)(2,1)} %collective-permute-done.21.refs_16_), channel_id=1, source_target_pairs={{0,16},{4,20},{8,24},{12,28},{16,0},{20,4},{24,8},{28,12},{1,17},{... | collective-permute-start | bytes 1572872 | tf_op jit(solution)/shard_map/ppermute | solution.py:422
  29.1 33.5 %collective-permute-start.15 = (bf16[1,2,1024,128]{3,2,1,0:T(8,128)(2,1)}, bf16[1,2,1024,128]{3,2,1,0:T(8,128)(2,1)S(1)}, u32[]{:S(2)}, u32[]{:S(2)}) collective-permute-start(bf16[1,2,1024,128]{3,2,1,0:T(8,128)(2,1)} %collective-permute-done.13.refs_8_), channel_id=1, source_target_pairs={{0,16},{4,20},{8,24},{12,28},{16,0},{20,4},{24,8},{28,12},{1,17},{... | collective-permute-start | bytes 1572872 | tf_op jit(solution)/shard_map/ppermute | solution.py:422
  34.5 29.4 %collective-permute-start.29 = (bf16[1,2,1024,128]{3,2,1,0:T(8,128)(2,1)}, bf16[1,2,1024,128]{3,2,1,0:T(8,128)(2,1)S(1)}, u32[]{:S(2)}, u32[]{:S(2)}) collective-permute-start(bf16[1,2,1024,128]{3,2,1,0:T(8,128)(2,1)} %collective-permute-done.13.refs_8_), channel_id=1, source_target_pairs={{1,2},{2,3},{5,6},{6,7},{9,10},{10,11},{13,14},{14,15},{17,18},{18... | collective-permute-start | bytes 1572872 | tf_op jit(solution)/shard_map/ppermute | solution.py:404
  47.6 19.7 %collective-permute-start.30 = (bf16[1,2,1024,128]{3,2,1,0:T(8,128)(2,1)}, bf16[1,2,1024,128]{3,2,1,0:T(8,128)(2,1)S(1)}, u32[]{:S(2)}, u32[]{:S(2)}) collective-permute-start(bf16[1,2,1024,128]{3,2,1,0:T(8,128)(2,1)} %collective-permute-done.21.refs_16_), channel_id=1, source_target_pairs={{1,0},{2,1},{5,4},{6,5},{9,8},{10,9},{13,12},{14,13},{17,16},{18,1... | collective-permute-start | bytes 1572872 | tf_op jit(solution)/shard_map/ppermute | solution.py:404
  48.3 19.1 %collective-permute-start.2 = (bf16[256,1024]{1,0:T(8,128)(2,1)S(1)}, bf16[256,1024]{1,0:T(8,128)(2,1)S(1)}, u32[]{:S(2)}, u32[]{:S(2)}) collective-permute-start(bf16[256,1024]{1,0:T(8,128)(2,1)S(1)} %collective-permute-done.refs_1_), channel_id=1, source_target_pairs={{1,2},{2,3},{5,6},{6,7},{9,10},{10,11},{13,14},{14,15},{17,18},{18... | collective-permute-start | bytes 1572872 | tf_op jit(solution)/shard_map/ppermute | solution.py:404
  49.6 19.3 %collective-permute-start.3 = (bf16[256,1024]{1,0:T(8,128)(2,1)S(1)}, bf16[256,1024]{1,0:T(8,128)(2,1)S(1)}, u32[]{:S(2)}, u32[]{:S(2)}) collective-permute-start(bf16[256,1024]{1,0:T(8,128)(2,1)S(1)} %collective-permute-done.1.refs_2_), channel_id=1, source_target_pairs={{1,0},{2,1},{5,4},{6,5},{9,8},{10,9},{13,12},{14,13},{17,16},{18,1... | collective-permute-start | bytes 1572872 | tf_op jit(solution)/shard_map/ppermute | solution.py:404
  73.6 17.9 %collective-permute-start.11 = (bf16[1,2,1024,128]{3,2,1,0:T(8,128)(2,1)}, bf16[1,2,1024,128]{3,2,1,0:T(8,128)(2,1)S(1)}, u32[]{:S(2)}, u32[]{:S(2)}) collective-permute-start(bf16[1,2,1024,128]{3,2,1,0:T(8,128)(2,1)} %collective-permute-done.7.refs_2_), channel_id=1, source_target_pairs={{0,4},{4,0},{8,12},{12,8},{16,20},{20,16},{24,28},{28,24},{1,5},{5... | collective-permute-start | bytes 1572872 | tf_op jit(solution)/shard_map/ppermute | solution.py:423
  80.2 19.6 %collective-permute-start.26 = (bf16[1,2,1024,128]{3,2,1,0:T(8,128)(2,1)S(1)}, bf16[1,2,1024,128]{3,2,1,0:T(8,128)(2,1)S(1)}, u32[]{:S(2)}, u32[]{:S(2)}) collective-permute-start(bf16[1,2,1024,128]{3,2,1,0:T(8,128)(2,1)S(1)} %collective-permute-done.22.refs_17_), channel_id=1, source_target_pairs={{0,4},{4,0},{8,12},{12,8},{16,20},{20,16},{24,28},{28,24},{1,5},{5... | collective-permute-start | bytes 1572872 | tf_op jit(solution)/shard_map/ppermute | solution.py:423
  91.5 24.2 %collective-permute-start.31 = (bf16[1,2,1024,128]{3,2,1,0:T(8,128)(2,1)S(1)}, bf16[1,2,1024,128]{3,2,1,0:T(8,128)(2,1)S(1)}, u32[]{:S(2)}, u32[]{:S(2)}) collective-permute-start(bf16[1,2,1024,128]{3,2,1,0:T(8,128)(2,1)S(1)} %broadcast_select_fusion.refs_0_), channel_id=1, source_target_pairs={{0,16},{4,20},{8,24},{12,28},{16,0},{20,4},{24,8},{28,12},{1,17},{... | collective-permute-start | bytes 1572872 | tf_op jit(solution)/shard_map/ppermute | solution.py:422
  93.1 21.7 %collective-permute-start.19 = (bf16[1,2,1024,128]{3,2,1,0:T(8,128)(2,1)S(1)}, bf16[1,2,1024,128]{3,2,1,0:T(8,128)(2,1)S(1)}, u32[]{:S(2)}, u32[]{:S(2)}) collective-permute-start(bf16[1,2,1024,128]{3,2,1,0:T(8,128)(2,1)S(1)} %collective-permute-done.15.refs_10_), channel_id=1, source_target_pairs={{0,4},{4,0},{8,12},{12,8},{16,20},{20,16},{24,28},{28,24},{1,5},{5... | collective-permute-start | bytes 1572872 | tf_op jit(solution)/shard_map/ppermute | solution.py:423
  93.4 21.7 %collective-permute-start.27 = (bf16[1,2,1024,128]{3,2,1,0:T(8,128)(2,1)S(1)}, bf16[1,2,1024,128]{3,2,1,0:T(8,128)(2,1)S(1)}, u32[]{:S(2)}, u32[]{:S(2)}) collective-permute-start(bf16[1,2,1024,128]{3,2,1,0:T(8,128)(2,1)S(1)} %collective-permute-done.23.refs_18_), channel_id=1, source_target_pairs={{0,4},{4,0},{8,12},{12,8},{16,20},{20,16},{24,28},{28,24},{1,5},{5... | collective-permute-start | bytes 1572872 | tf_op jit(solution)/shard_map/ppermute | solution.py:423
  93.6 22.4 %collective-permute-start.4 = (bf16[256,1024]{1,0:T(8,128)(2,1)S(1)}, bf16[256,1024]{1,0:T(8,128)(2,1)S(1)}, u32[]{:S(2)}, u32[]{:S(2)}) collective-permute-start(bf16[256,1024]{1,0:T(8,128)(2,1)S(1)} %get-tuple-element.23), channel_id=1, source_target_pairs={{0,1},{1,2},{2,3},{3,4},{4,5},{5,6},{6,7},{7,8},{8,9},{9,10},{10,1... | collective-permute-start | bytes 1572872 | tf_op jit(solution)/shard_map/ppermute | solution.py:441
  99.7 28.2 %collective-permute-start.5 = (bf16[256,1024]{1,0:T(8,128)(2,1)S(1)}, bf16[256,1024]{1,0:T(8,128)(2,1)S(1)}, u32[]{:S(2)}, u32[]{:S(2)}) collective-permute-start(bf16[256,1024]{1,0:T(8,128)(2,1)S(1)} %get-tuple-element.24), channel_id=1, source_target_pairs={{1,0},{2,1},{3,2},{4,3},{5,4},{6,5},{7,6},{8,7},{9,8},{10,9},{11,1... | collective-permute-start | bytes 1572872 | tf_op jit(solution)/shard_map/ppermute | solution.py:442
  114.7 25.1 %collective-permute-start.32 = (bf16[1,2,1024,128]{3,2,1,0:T(8,128)(2,1)S(1)}, bf16[1,2,1024,128]{3,2,1,0:T(8,128)(2,1)S(1)}, u32[]{:S(2)}, u32[]{:S(2)}) collective-permute-start(bf16[1,2,1024,128]{3,2,1,0:T(8,128)(2,1)S(1)} %broadcast_select_fusion.refs_0_), channel_id=1, source_target_pairs={{0,8},{4,12},{8,0},{12,4},{16,24},{20,28},{24,16},{28,20},{1,9},{5... | collective-permute-start | bytes 1572872 | tf_op jit(solution)/shard_map/ppermute | solution.py:422
  115.1 24.7 %collective-permute-start.12 = (bf16[1,2,1024,128]{3,2,1,0:T(8,128)(2,1)S(1)}, bf16[1,2,1024,128]{3,2,1,0:T(8,128)(2,1)S(1)}, u32[]{:S(2)}, u32[]{:S(2)}) collective-permute-start(bf16[1,2,1024,128]{3,2,1,0:T(8,128)(2,1)S(1)} %collective-permute-done.8.refs_3_), channel_id=1, source_target_pairs={{0,4},{4,0},{8,12},{12,8},{16,20},{20,16},{24,28},{28,24},{1,5},{5... | collective-permute-start | bytes 1572872 | tf_op jit(solution)/shard_map/ppermute | solution.py:423
  115.6 24.7 %collective-permute-start.20 = (bf16[1,2,1024,128]{3,2,1,0:T(8,128)(2,1)S(1)}, bf16[1,2,1024,128]{3,2,1,0:T(8,128)(2,1)S(1)}, u32[]{:S(2)}, u32[]{:S(2)}) collective-permute-start(bf16[1,2,1024,128]{3,2,1,0:T(8,128)(2,1)S(1)} %collective-permute-done.16.refs_11_), channel_id=1, source_target_pairs={{0,4},{4,0},{8,12},{12,8},{16,20},{20,16},{24,28},{28,24},{1,5},{5... | collective-permute-start | bytes 1572872 | tf_op jit(solution)/shard_map/ppermute | solution.py:423
  116.0 29.9 %collective-permute-start.28 = (bf16[1,2,1024,128]{3,2,1,0:T(8,128)(2,1)S(1)}, bf16[1,2,1024,128]{3,2,1,0:T(8,128)(2,1)S(1)}, u32[]{:S(2)}, u32[]{:S(2)}) collective-permute-start(bf16[1,2,1024,128]{3,2,1,0:T(8,128)(2,1)S(1)} %collective-permute-done.24.refs_19_), channel_id=1, source_target_pairs={{0,4},{4,0},{8,12},{12,8},{16,20},{20,16},{24,28},{28,24},{1,5},{5... | collective-permute-start | bytes 1572872 | tf_op jit(solution)/shard_map/ppermute | solution.py:423
  127.9 17.2 %collective-permute-start.33 = (bf16[1,2,1024,128]{3,2,1,0:T(8,128)(2,1)S(1)}, bf16[1,2,1024,128]{3,2,1,0:T(8,128)(2,1)S(1)}, u32[]{:S(2)}, u32[]{:S(2)}) collective-permute-start(bf16[1,2,1024,128]{3,2,1,0:T(8,128)(2,1)S(1)} %collective-permute-done.31.refs_1_), channel_id=1, source_target_pairs={{0,8},{4,12},{8,0},{12,4},{16,24},{20,28},{24,16},{28,20},{1,9},{5... | collective-permute-start | bytes 1572872 | tf_op jit(solution)/shard_map/ppermute | solution.py:422
  (22 other events, 357.4 us)

commit v2 on v1

--- a/solution.py
+++ b/solution.py
@@ -84,11 +84,16 @@
     return peak, mixed, total
 
 
-def merge(first, second):
+def combine(first, second):
     peak = jnp.maximum(first[0], second[0])
     left, right = jnp.exp(first[0] - peak), jnp.exp(second[0] - peak)
     mixed = first[1] * left + second[1] * right
     total = first[2] * left + second[2] * right
+    return peak, mixed, total
+
+
+def merge(first, second):
+    _, mixed, total = combine(first, second)
     return mixed / total
 
 
@@ -115,8 +120,8 @@
         base += size
 
 
-def cross_head_kernel(width, query, w_kv, *refs):
-    chunks, (peak, mixed, total, keys, values, bias) = refs[:-6], refs[-6:]
+def cross_head_kernel(width, count, query, w_kv, *refs):
+    chunks, known, (peak, mixed, total, keys, values, bias) = refs[:count], refs[count:-6], refs[-6:]
     nodes, feat = query.shape
     project_observations(chunks, w_kv, keys, values, bias)
     sides = head_sides(width)
@@ -129,9 +134,10 @@
         @pl.loop(0, nodes // step)
         def _(block):
             part = pl.ds(pl.multiple_of(block * step, step), step)
-            peak[part, at], mixed[part, at], total[part, at] = softmax_part(
-                query[part, at], keys[:, at], values[:, at], sides, bias[...]
-            )
+            state = softmax_part(query[part, at], keys[:, at], values[:, at], sides, bias[...])
+            if known:
+                state = combine([ref[part, at] for ref in known], state)
+            peak[part, at], mixed[part, at], total[part, at] = state
 
 
 def cross_tail_kernel(
@@ -158,25 +164,31 @@
     last[...] = after[nodes - last.shape[0] :]
 
 
-def cross_attention(latent, queries, rows, w_kv, w_out, half):
-    nodes, feat = latent.shape
-    width = feat // HEADS
-    chunks, last = rows[:-1], rows[-1]
+def cross_head(queries, w_kv, chunks, known):
+    nodes, feat = queries.shape
     size = sum(chunk.shape[0] for chunk in chunks)
-    state = pl.pallas_call(
-        functools.partial(cross_head_kernel, width),
+    return pl.pallas_call(
+        functools.partial(cross_head_kernel, feat // HEADS, len(chunks)),
         out_shape=[jax.ShapeDtypeStruct((nodes, feat), F32)] * 3,
-        in_specs=[vmem()] * (2 + len(chunks)),
+        in_specs=[vmem()] * (2 + len(chunks) + len(known)),
         out_specs=[vmem()] * 3,
         scratch_shapes=[
             pltpu.VMEM((size, feat), BF16),
             pltpu.VMEM((size, feat), BF16),
             pltpu.VMEM((size, LANES), BF16),
         ],
-        compiler_params=params(min(60, 14 + 16 * size // 1024)),
-        cost_estimate=pl.CostEstimate(flops=16_000_000_000, bytes_accessed=12 << 20, transcendentals=0),
-        name="cross_head",
-    )(queries, w_kv, *chunks)
+        compiler_params=params(min(60, 16 + 16 * size // 1024)),
+        cost_estimate=pl.CostEstimate(flops=16_000_000 * size, bytes_accessed=12 << 20, transcendentals=0),
+    )(queries, w_kv, *chunks, *known)
+
+
+def cross_attention(latent, queries, rows, w_kv, w_out, half):
+    nodes, feat = latent.shape
+    width = feat // HEADS
+    first, *chunks, last = rows
+    state = cross_head(queries, w_kv, [first], ())
+    if chunks:
+        state = cross_head(queries, w_kv, chunks, state)
     size = last.shape[0]
     return pl.pallas_call(
         functools.partial(cross_tail_kernel, width),

time: 157 us -> 155 us (0.987)
  the two profiles are of different devices: /device:TPU:25 before, /device:TPU:0 now
where the time goes in v2:
time: 155 us; the launch traced here: 152 us
  Pallas kernels  55.6 us (36%)
  starting transfers between devices  45.6 us (29%)
  waiting for transfers between devices  40.9 us (26%)
  other arithmetic  4.35 us (3%)
  local copies, waits for them, and re-layouts  3.36 us (2%)
  matrix products  1.91 us (1%)
    ppermute x12, starting transfers between devices, spread(): parts.append(lax.ppermute(part, 'loc', flip[mask]))  20.3 us
    pallas_call x2, Pallas kernels, cross_head(): pl.pallas_call(functools.partial(cross_head_kernel, feat // HEADS, len(ch...  18.5 us
    pallas_call x2, Pallas kernels, mlp(): pl.pallas_call(functools.partial(mlp_kernel, group), out_shape=jax.ShapeD...  10.7 us
    ppermute x1, waiting for transfers between devices, shards(): high = lax.ppermute(first, everyone, [(i + 1, i) for i in range(count - 1)])  10.4 us
    all_to_all x1, waiting for transfers between devices, shards(): lax.all_to_all(marked, 'loc', split_axis=2, concat_axis=1, tiled=True)  9.7 us
    ppermute x4, waiting for transfers between devices, pass_on(): return lax.ppermute(value, 'stream', pairs)  9.67 us
    pallas_call x1, Pallas kernels, window_halo(): pl.pallas_call(functools.partial(window_halo_kernel, feat // HEADS), out_...  9.67 us
    pallas_call x1, Pallas kernels, window_local(): pl.pallas_call(functools.partial(window_local_kernel, feat // HEADS, half...  9 us
  transfers between devices with their start and end apart: 39, of which 10 were waited for; matrix products, arithmetic and copies ran while one was open for 3% of the time, Pallas kernels for 34%

profile of v2, /device:TPU:0, one launch (start us, length us, event | category | flops | bytes accessed | tf_op | source)
XLA Modules:
  0.0 152.3 jit_solution(7963572926874051208)
XLA Ops:
  1.2 3.1 %collective-permute-start.13 = (bf16[1,2,1024,128]{3,2,1,0:T(8,128)(2,1)S(1)}, bf16[1,2,1024,128]{3,2,1,0:T(8,128)(2,1)}, u32[]{:S(2)}, u32[]{:S(2)}) collective-permute-start(bf16[1,2,1024,128]{3,2,1,0:T(8,128)(2,1)S(1)} %maximum_bitcast_fusion.refs_0_), channel_id=1, source_target_pairs={{0,1},{1,2},{2,3},{3,0},{4,5},{5,6},{6,7},{7,4},{8,9},{9,10},{10,1... | collective-permute-start | bytes 1572872 | tf_op jit(solution)/shard_map/ppermute | solution.py:412
  4.3 2.1 %collective-permute-start.21 = (bf16[1,2,1024,128]{3,2,1,0:T(8,128)(2,1)S(1)}, bf16[1,2,1024,128]{3,2,1,0:T(8,128)(2,1)}, u32[]{:S(2)}, u32[]{:S(2)}) collective-permute-start(bf16[1,2,1024,128]{3,2,1,0:T(8,128)(2,1)S(1)} %maximum_bitcast_fusion.refs_0_), channel_id=1, source_target_pairs={{0,3},{1,0},{2,1},{3,2},{4,7},{5,4},{6,5},{7,6},{8,11},{9,8},{10,9... | collective-permute-start | bytes 1572872 | tf_op jit(solution)/shard_map/ppermute | solution.py:412
  12.3 4.1 %all-to-all-start = ((bf16[1,1,8,32,1024]{4,3,1,0,2:T(8,128)(2,1)}), bf16[1,1,8,32,1024]{4,3,1,0,2:T(8,128)(2,1)}, u32[]{:S(2)}, u32[]{:S(2)}) async-start(bf16[1,1,8,32,1024]{4,3,1,0,2:T(8,128)(2,1)} %bitcast_select_fusion), calls=%async_computation | async-start | bytes 1048576 | tf_op jit(solution)/shard_map/all_to_all | solution.py:447
  17.1 9.7 %all-to-all-done = bf16[1,1,8,32,1024]{4,3,1,0,2:T(8,128)(2,1)} async-done(((bf16[1,1,8,32,1024]{4,3,1,0,2:T(8,128)(2,1)}), bf16[1,1,8,32,1024]{4,3,1,0,2:T(8,128)(2,1)}, u32[]{:S(2)}, u32[]{:S(2)}) %all-to-all-start) | async-done | bytes 524320 | tf_op jit(solution)/shard_map/all_to_all | solution.py:447
  26.8 2.3 %collective-permute-done.21.refs_16_ = bf16[1,2,1024,128]{3,2,1,0:T(8,128)(2,1)} collective-permute-done((bf16[1,2,1024,128]{3,2,1,0:T(8,128)(2,1)S(1)}, bf16[1,2,1024,128]{3,2,1,0:T(8,128)(2,1)}, u32[]{:S(2)}, u32[]{:S(2)}) %collective-permute-start.21) | collective-permute-done | bytes 524320 | tf_op jit(solution)/shard_map/ppermute | solution.py:412
  29.1 3.3 %collective-permute-start.1 = (bf16[256,1024]{1,0:T(8,128)(2,1)}, bf16[256,1024]{1,0:T(8,128)(2,1)}, u32[]{:S(2)}, u32[]{:S(2)}) collective-permute-start(bf16[256,1024]{1,0:T(8,128)(2,1)} %bitcast.4.refs_0_), channel_id=1, source_target_pairs={{0,3},{1,0},{2,1},{3,2},{4,7},{5,4},{6,5},{7,6},{8,11},{9,8},{10,9... | collective-permute-start | bytes 1572872 | tf_op jit(solution)/shard_map/ppermute | solution.py:412
  37.2 2.2 %copy-done.2 = bf16[1024,2048]{1,0:T(8,128)(2,1)S(1)} copy-done((bf16[1024,2048]{1,0:T(8,128)(2,1)S(1)}, bf16[1024,2048]{1,0:T(8,128)(2,1)}, u32[]{:S(2)}) %copy-start.2) | copy-done | bytes 4194328
  40.5 8.9 %shard_map.100 = (f32[384,1024]{1,0:T(8,128)S(1)}, f32[384,1024]{1,0:T(8,128)S(1)}, f32[384,1024]{1,0:T(8,128)S(1)}) custom-call(bf16[384,1024]{1,0:T(8,128)(2,1)S(1)} %copy-done.6, bf16[1024,2048]{1,0:T(8,128)(2,1)S(1)} %copy-done.2, bf16[256,1024]{1,0:T(8,128)(2,1)} %bitcast.4.refs_0_), custom_call_target="tpu_custom_call" | custom-call | flops 4096000000 | bytes 12582912 | tf_op jit(solution)/shard_map/pallas_call | solution.py:170
  55.7 9.7 %shard_map.101 = (f32[384,1024]{1,0:T(8,128)S(1)}, f32[384,1024]{1,0:T(8,128)S(1)}, f32[384,1024]{1,0:T(8,128)S(1)}) custom-call(bf16[384,1024]{1,0:T(8,128)(2,1)S(1)} %copy-done.7, bf16[1024,2048]{1,0:T(8,128)(2,1)S(1)} %copy-done.3, bf16[256,1024]{1,0:T(8,128)(2,1)} %collective-permute-done.refs_0_, bf16[256,1024]{1,0:T(8,128)(2,1)} %collective-permute-done.1.refs_1_, ...), custom_call_target="tpu_custom_call" | custom-call | flops 8192000000 | bytes 12582912 | tf_op jit(solution)/shard_map/pallas_call | solution.py:170
  66.9 2.1 %collective-permute-done.30 = bf16[1,2,1024,128]{3,2,1,0:T(8,128)(2,1)S(1)} collective-permute-done((bf16[1,2,1024,128]{3,2,1,0:T(8,128)(2,1)}, bf16[1,2,1024,128]{3,2,1,0:T(8,128)(2,1)S(1)}, u32[]{:S(2)}, u32[]{:S(2)}) %collective-permute-start.30) | collective-permute-done | bytes 524320 | tf_op jit(solution)/shard_map/ppermute | solution.py:416
  69.0 2.7 %collective-permute-start.8 = (bf16[1,2,1024,128]{3,2,1,0:T(8,128)(2,1)}, bf16[1,2,1024,128]{3,2,1,0:T(8,128)(2,1)S(1)}, u32[]{:S(2)}, u32[]{:S(2)}) collective-permute-start(bf16[1,2,1024,128]{3,2,1,0:T(8,128)(2,1)} %collective-permute-done.6.refs_1_), channel_id=1, source_target_pairs={{0,16},{4,20},{8,24},{12,28},{16,0},{20,4},{24,8},{28,12},{1,17},{... | collective-permute-start | bytes 1572872 | tf_op jit(solution)/shard_map/ppermute | solution.py:434
  71.8 7.6 %collective-permute-done.3 = bf16[256,1024]{1,0:T(8,128)(2,1)S(1)} collective-permute-done((bf16[256,1024]{1,0:T(8,128)(2,1)}, bf16[256,1024]{1,0:T(8,128)(2,1)S(1)}, u32[]{:S(2)}, u32[]{:S(2)}) %collective-permute-start.3) | collective-permute-done | bytes 524320 | tf_op jit(solution)/shard_map/ppermute | solution.py:416
  80.1 2.7 %collective-permute-start.16 = (bf16[1,2,1024,128]{3,2,1,0:T(8,128)(2,1)}, bf16[1,2,1024,128]{3,2,1,0:T(8,128)(2,1)S(1)}, u32[]{:S(2)}, u32[]{:S(2)}) collective-permute-start(bf16[1,2,1024,128]{3,2,1,0:T(8,128)(2,1)} %collective-permute-done.14.refs_9_), channel_id=1, source_target_pairs={{0,16},{4,20},{8,24},{12,28},{16,0},{20,4},{24,8},{28,12},{1,17},{... | collective-permute-start | bytes 1572872 | tf_op jit(solution)/shard_map/ppermute | solution.py:434
  82.8 2.0 %collective-permute-done.8.refs_3_ = bf16[1,2,1024,128]{3,2,1,0:T(8,128)(2,1)S(1)} collective-permute-done((bf16[1,2,1024,128]{3,2,1,0:T(8,128)(2,1)}, bf16[1,2,1024,128]{3,2,1,0:T(8,128)(2,1)S(1)}, u32[]{:S(2)}, u32[]{:S(2)}) %collective-permute-start.8) | collective-permute-done | bytes 524320 | tf_op jit(solution)/shard_map/ppermute | solution.py:434
  85.6 7.7 %cross_tail.1 = (bf16[384,1024]{1,0:T(8,128)(2,1)S(1)}, bf16[256,1024]{1,0:T(8,128)(2,1)S(1)}, bf16[256,1024]{1,0:T(8,128)(2,1)S(1)}) custom-call(bf16[384,1024]{1,0:T(8,128)(2,1)S(1)} %copy-done.1, bf16[384,1024]{1,0:T(8,128)(2,1)S(1)} %copy-done.7, bf16[1024,2048]{1,0:T(8,128)(2,1)S(1)} %copy-done.3, bf16[1024,1024]{1,0:T(8,128)(2,1)S(1)} %copy-done.4, ...), custom_call_target="tpu_custom_call" | custom-call | flops 7000000000 | bytes 12582912 | tf_op jit(solution)/shard_map/cross_tail/pallas_call | solution.py:193
  95.8 2.7 %collective-permute-done.24.refs_19_ = bf16[1,2,1024,128]{3,2,1,0:T(8,128)(2,1)S(1)} collective-permute-done((bf16[1,2,1024,128]{3,2,1,0:T(8,128)(2,1)}, bf16[1,2,1024,128]{3,2,1,0:T(8,128)(2,1)S(1)}, u32[]{:S(2)}, u32[]{:S(2)}) %collective-permute-start.24) | collective-permute-done | bytes 524320 | tf_op jit(solution)/shard_map/ppermute | solution.py:434
  98.5 4.9 %collective-permute-start.4 = (bf16[256,1024]{1,0:T(8,128)(2,1)S(1)}, bf16[256,1024]{1,0:T(8,128)(2,1)S(1)}, u32[]{:S(2)}, u32[]{:S(2)}) collective-permute-start(bf16[256,1024]{1,0:T(8,128)(2,1)S(1)} %get-tuple-element.29), channel_id=1, source_target_pairs={{0,1},{1,2},{2,3},{3,4},{4,5},{5,6},{6,7},{7,8},{8,9},{9,10},{10,1... | collective-permute-start | bytes 1572872 | tf_op jit(solution)/shard_map/ppermute | solution.py:453
  104.8 9.0 %window_local.1 = (bf16[384,1024]{1,0:T(8,128)(2,1)S(1)}, f32[384,1024]{1,0:T(8,128)S(1)}, f32[384,1024]{1,0:T(8,128)S(1)}, f32[384,1024]{1,0:T(8,128)S(1)}) custom-call(bf16[384,1024]{1,0:T(8,128)(2,1)S(1)} %get-tuple-element.24.own, bf16[1024,3072]{1,0:T(8,128)(2,1)S(1)} %bitcast.12), custom_call_target="tpu_custom_call" | custom-call | flops 15000000512 | bytes 12582912 | tf_op jit(solution)/shard_map/window_local/pallas_call | solution.py:286
  113.8 2.4 %collective-permute-start.32 = (bf16[1,2,1024,128]{3,2,1,0:T(8,128)(2,1)S(1)}, bf16[1,2,1024,128]{3,2,1,0:T(8,128)(2,1)S(1)}, u32[]{:S(2)}, u32[]{:S(2)}) collective-permute-start(bf16[1,2,1024,128]{3,2,1,0:T(8,128)(2,1)S(1)} %broadcast_select_fusion.refs_0_), channel_id=1, source_target_pairs={{0,8},{4,12},{8,0},{12,4},{16,24},{20,28},{24,16},{28,20},{1,9},{5... | collective-permute-start | bytes 1572872 | tf_op jit(solution)/shard_map/ppermute | solution.py:434
  117.0 10.4 %collective-permute-done.5.high = bf16[256,1024]{1,0:T(8,128)(2,1)S(1)} collective-permute-done((bf16[256,1024]{1,0:T(8,128)(2,1)S(1)}, bf16[256,1024]{1,0:T(8,128)(2,1)S(1)}, u32[]{:S(2)}, u32[]{:S(2)}) %collective-permute-start.5) | collective-permute-done | bytes 524320 | tf_op jit(solution)/shard_map/ppermute | solution.py:454
  128.9 9.7 %window_halo.1.rows.base = bf16[384,1024]{1,0:T(8,128)(2,1)S(1)} custom-call(f32[2]{0:T(128)S(1)} %add_select_fusion.edge, bf16[384,1024]{1,0:T(8,128)(2,1)S(1)} %get-tuple-element.24.own, bf16[384,1024]{1,0:T(8,128)(2,1)S(1)} %get-tuple-element.25.query, f32[384,1024]{1,0:T(8,128)S(1)} %get-tuple-element.26.peak, f32[384,1024]{1,0:T(8,128)S(1)} %get-tuple-element.27.mixed, ...), custom_call_target="tpu_custom_call" | custom-call | flops 10000000000 | bytes 12582912 | tf_op jit(solution)/shard_map/window_halo/pallas_call | solution.py:301
  139.3 2.0 %collective-permute-done.33.refs_3_ = bf16[1,2,1024,128]{3,2,1,0:T(8,128)(2,1)S(1)} collective-permute-done((bf16[1,2,1024,128]{3,2,1,0:T(8,128)(2,1)S(1)}, bf16[1,2,1024,128]{3,2,1,0:T(8,128)(2,1)S(1)}, u32[]{:S(2)}, u32[]{:S(2)}) %collective-permute-start.33) | collective-permute-done | bytes 524320 | tf_op jit(solution)/shard_map/ppermute | solution.py:434
  141.3 7.2 %shard_map.102.base = f32[384,1024]{1,0:T(8,128)S(1)} custom-call(bf16[384,1024]{1,0:T(8,128)(2,1)S(1)} %window_halo.1.rows.base, bf16[384,1024]{1,0:T(8,128)(2,1)S(1)} %window_halo.1.rows.base, bf16[1,2,1024,128]{3,2,1,0:T(8,128)(2,1)S(1)} %maximum_bitcast_fusion.refs_0_, bf16[1,2,1024,128]{3,2,1,0:T(8,128)(2,1)} %collective-permute-done.6.refs_1_, ...), custom_call_target="tpu_custom_call" | custom-call | flops 6000000000 | bytes 12582912 | tf_op jit(solution)/shard_map/pallas_call | solution.py:376
  148.5 3.6 %shard_map.103 = bf16[384,1024]{1,0:T(8,128)(2,1)} custom-call(bf16[384,1024]{1,0:T(8,128)(2,1)S(1)} %window_halo.1.rows.base, f32[384,1024]{1,0:T(8,128)S(1)} %shard_map.102.base, bf16[1,2,1024,128]{3,2,1,0:T(8,128)(2,1)S(1)} %broadcast_select_fusion.refs_0_, bf16[1,2,1024,128]{3,2,1,0:T(8,128)(2,1)S(1)} %collective-permute-done.31.refs_1_, ...), custom_call_target="tpu_custom_call" | custom-call | flops 6000000000 | bytes 12582912 | tf_op jit(solution)/shard_map/pallas_call | solution.py:376
  (91 shorter events, 29.8 us)
Async XLA Ops:
  1.2 25.5 %collective-permute-start.13 = (bf16[1,2,1024,128]{3,2,1,0:T(8,128)(2,1)S(1)}, bf16[1,2,1024,128]{3,2,1,0:T(8,128)(2,1)}, u32[]{:S(2)}, u32[]{:S(2)}) collective-permute-start(bf16[1,2,1024,128]{3,2,1,0:T(8,128)(2,1)S(1)} %maximum_bitcast_fusion.refs_0_), channel_id=1, source_target_pairs={{0,1},{1,2},{2,3},{3,0},{4,5},{5,6},{6,7},{7,4},{8,9},{9,10},{10,1... | collective-permute-start | bytes 1572872 | tf_op jit(solution)/shard_map/ppermute | solution.py:412
  4.3 24.7 %collective-permute-start.21 = (bf16[1,2,1024,128]{3,2,1,0:T(8,128)(2,1)S(1)}, bf16[1,2,1024,128]{3,2,1,0:T(8,128)(2,1)}, u32[]{:S(2)}, u32[]{:S(2)}) collective-permute-start(bf16[1,2,1024,128]{3,2,1,0:T(8,128)(2,1)S(1)} %maximum_bitcast_fusion.refs_0_), channel_id=1, source_target_pairs={{0,3},{1,0},{2,1},{3,2},{4,7},{5,4},{6,5},{7,6},{8,11},{9,8},{10,9... | collective-permute-start | bytes 1572872 | tf_op jit(solution)/shard_map/ppermute | solution.py:412
  6.4 25.9 %collective-permute-start.6 = (bf16[1,2,1024,128]{3,2,1,0:T(8,128)(2,1)S(1)}, bf16[1,2,1024,128]{3,2,1,0:T(8,128)(2,1)}, u32[]{:S(2)}, u32[]{:S(2)}) collective-permute-start(bf16[1,2,1024,128]{3,2,1,0:T(8,128)(2,1)S(1)} %maximum_bitcast_fusion.refs_0_), channel_id=1, source_target_pairs={{0,8},{4,12},{8,0},{12,4},{16,24},{20,28},{24,16},{28,20},{1,9},{5... | collective-permute-start | bytes 1572872 | tf_op jit(solution)/shard_map/ppermute | solution.py:434
  8.1 25.7 %collective-permute-start.7 = (bf16[1,2,1024,128]{3,2,1,0:T(8,128)(2,1)S(1)}, bf16[1,2,1024,128]{3,2,1,0:T(8,128)(2,1)}, u32[]{:S(2)}, u32[]{:S(2)}) collective-permute-start(bf16[1,2,1024,128]{3,2,1,0:T(8,128)(2,1)S(1)} %maximum_bitcast_fusion.refs_0_), channel_id=1, source_target_pairs={{0,16},{4,20},{8,24},{12,28},{16,0},{20,4},{24,8},{28,12},{1,17},{... | collective-permute-start | bytes 1572872 | tf_op jit(solution)/shard_map/ppermute | solution.py:434
  16.4 33.0 %collective-permute-start.9 = (bf16[1,2,1024,128]{3,2,1,0:T(8,128)(2,1)S(1)}, bf16[1,2,1024,128]{3,2,1,0:T(8,128)(2,1)}, u32[]{:S(2)}, u32[]{:S(2)}) collective-permute-start(bf16[1,2,1024,128]{3,2,1,0:T(8,128)(2,1)S(1)} %maximum_bitcast_fusion.refs_0_), channel_id=1, source_target_pairs={{0,4},{4,0},{8,12},{12,8},{16,20},{20,16},{24,28},{28,24},{1,5},{5... | collective-permute-start | bytes 1572872 | tf_op jit(solution)/shard_map/ppermute | solution.py:435
  26.8 23.4 %collective-permute-start = (bf16[256,1024]{1,0:T(8,128)(2,1)}, bf16[256,1024]{1,0:T(8,128)(2,1)}, u32[]{:S(2)}, u32[]{:S(2)}) collective-permute-start(bf16[256,1024]{1,0:T(8,128)(2,1)} %bitcast.4.refs_0_), channel_id=1, source_target_pairs={{0,1},{1,2},{2,3},{3,0},{4,5},{5,6},{6,7},{7,4},{8,9},{9,10},{10,1... | collective-permute-start | bytes 1572872 | tf_op jit(solution)/shard_map/ppermute | solution.py:412
  29.1 23.1 %collective-permute-start.1 = (bf16[256,1024]{1,0:T(8,128)(2,1)}, bf16[256,1024]{1,0:T(8,128)(2,1)}, u32[]{:S(2)}, u32[]{:S(2)}) collective-permute-start(bf16[256,1024]{1,0:T(8,128)(2,1)} %bitcast.4.refs_0_), channel_id=1, source_target_pairs={{0,3},{1,0},{2,1},{3,2},{4,7},{5,4},{6,5},{7,6},{8,11},{9,8},{10,9... | collective-permute-start | bytes 1572872 | tf_op jit(solution)/shard_map/ppermute | solution.py:412
  32.3 21.1 %collective-permute-start.14 = (bf16[1,2,1024,128]{3,2,1,0:T(8,128)(2,1)}, bf16[1,2,1024,128]{3,2,1,0:T(8,128)(2,1)}, u32[]{:S(2)}, u32[]{:S(2)}) collective-permute-start(bf16[1,2,1024,128]{3,2,1,0:T(8,128)(2,1)} %collective-permute-done.13.refs_8_), channel_id=1, source_target_pairs={{0,8},{4,12},{8,0},{12,4},{16,24},{20,28},{24,16},{28,20},{1,9},{5... | collective-permute-start | bytes 1572872 | tf_op jit(solution)/shard_map/ppermute | solution.py:434
  33.8 20.3 %collective-permute-start.22 = (bf16[1,2,1024,128]{3,2,1,0:T(8,128)(2,1)}, bf16[1,2,1024,128]{3,2,1,0:T(8,128)(2,1)}, u32[]{:S(2)}, u32[]{:S(2)}) collective-permute-start(bf16[1,2,1024,128]{3,2,1,0:T(8,128)(2,1)} %collective-permute-done.21.refs_16_), channel_id=1, source_target_pairs={{0,16},{4,20},{8,24},{12,28},{16,0},{20,4},{24,8},{28,12},{1,17},{... | collective-permute-start | bytes 1572872 | tf_op jit(solution)/shard_map/ppermute | solution.py:434
  49.4 15.9 %collective-permute-start.15 = (bf16[1,2,1024,128]{3,2,1,0:T(8,128)(2,1)}, bf16[1,2,1024,128]{3,2,1,0:T(8,128)(2,1)S(1)}, u32[]{:S(2)}, u32[]{:S(2)}) collective-permute-start(bf16[1,2,1024,128]{3,2,1,0:T(8,128)(2,1)} %collective-permute-done.13.refs_8_), channel_id=1, source_target_pairs={{0,16},{4,20},{8,24},{12,28},{16,0},{20,4},{24,8},{28,12},{1,17},{... | collective-permute-start | bytes 1572872 | tf_op jit(solution)/shard_map/ppermute | solution.py:434
  50.1 16.8 %collective-permute-start.29 = (bf16[1,2,1024,128]{3,2,1,0:T(8,128)(2,1)}, bf16[1,2,1024,128]{3,2,1,0:T(8,128)(2,1)S(1)}, u32[]{:S(2)}, u32[]{:S(2)}) collective-permute-start(bf16[1,2,1024,128]{3,2,1,0:T(8,128)(2,1)} %collective-permute-done.13.refs_8_), channel_id=1, source_target_pairs={{1,2},{2,3},{5,6},{6,7},{9,10},{10,11},{13,14},{14,15},{17,18},{18... | collective-permute-start | bytes 1572872 | tf_op jit(solution)/shard_map/ppermute | solution.py:416
  52.2 16.9 %collective-permute-start.30 = (bf16[1,2,1024,128]{3,2,1,0:T(8,128)(2,1)}, bf16[1,2,1024,128]{3,2,1,0:T(8,128)(2,1)S(1)}, u32[]{:S(2)}, u32[]{:S(2)}) collective-permute-start(bf16[1,2,1024,128]{3,2,1,0:T(8,128)(2,1)} %collective-permute-done.21.refs_16_), channel_id=1, source_target_pairs={{1,0},{2,1},{5,4},{6,5},{9,8},{10,9},{13,12},{14,13},{17,16},{18,1... | collective-permute-start | bytes 1572872 | tf_op jit(solution)/shard_map/ppermute | solution.py:416
  54.2 25.2 %collective-permute-start.3 = (bf16[256,1024]{1,0:T(8,128)(2,1)}, bf16[256,1024]{1,0:T(8,128)(2,1)S(1)}, u32[]{:S(2)}, u32[]{:S(2)}) collective-permute-start(bf16[256,1024]{1,0:T(8,128)(2,1)} %collective-permute-done.1.refs_1_), channel_id=1, source_target_pairs={{1,0},{2,1},{5,4},{6,5},{9,8},{10,9},{13,12},{14,13},{17,16},{18,1... | collective-permute-start | bytes 1572872 | tf_op jit(solution)/shard_map/ppermute | solution.py:416
  82.8 15.8 %collective-permute-start.18 = (bf16[1,2,1024,128]{3,2,1,0:T(8,128)(2,1)}, bf16[1,2,1024,128]{3,2,1,0:T(8,128)(2,1)S(1)}, u32[]{:S(2)}, u32[]{:S(2)}) collective-permute-start(bf16[1,2,1024,128]{3,2,1,0:T(8,128)(2,1)} %collective-permute-done.14.refs_9_), channel_id=1, source_target_pairs={{0,4},{4,0},{8,12},{12,8},{16,20},{20,16},{24,28},{28,24},{1,5},{5... | collective-permute-start | bytes 1572872 | tf_op jit(solution)/shard_map/ppermute | solution.py:435
  85.5 17.9 %collective-permute-start.26 = (bf16[1,2,1024,128]{3,2,1,0:T(8,128)(2,1)}, bf16[1,2,1024,128]{3,2,1,0:T(8,128)(2,1)S(1)}, u32[]{:S(2)}, u32[]{:S(2)}) collective-permute-start(bf16[1,2,1024,128]{3,2,1,0:T(8,128)(2,1)} %collective-permute-done.22.refs_17_), channel_id=1, source_target_pairs={{0,4},{4,0},{8,12},{12,8},{16,20},{20,16},{24,28},{28,24},{1,5},{5... | collective-permute-start | bytes 1572872 | tf_op jit(solution)/shard_map/ppermute | solution.py:435
  93.3 22.9 %collective-permute-start.31 = (bf16[1,2,1024,128]{3,2,1,0:T(8,128)(2,1)S(1)}, bf16[1,2,1024,128]{3,2,1,0:T(8,128)(2,1)S(1)}, u32[]{:S(2)}, u32[]{:S(2)}) collective-permute-start(bf16[1,2,1024,128]{3,2,1,0:T(8,128)(2,1)S(1)} %broadcast_select_fusion.refs_0_), channel_id=1, source_target_pairs={{0,16},{4,20},{8,24},{12,28},{16,0},{20,4},{24,8},{28,12},{1,17},{... | collective-permute-start | bytes 1572872 | tf_op jit(solution)/shard_map/ppermute | solution.py:434
  95.8 18.0 %collective-permute-start.19 = (bf16[1,2,1024,128]{3,2,1,0:T(8,128)(2,1)S(1)}, bf16[1,2,1024,128]{3,2,1,0:T(8,128)(2,1)S(1)}, u32[]{:S(2)}, u32[]{:S(2)}) collective-permute-start(bf16[1,2,1024,128]{3,2,1,0:T(8,128)(2,1)S(1)} %collective-permute-done.15.refs_10_), channel_id=1, source_target_pairs={{0,4},{4,0},{8,12},{12,8},{16,20},{20,16},{24,28},{28,24},{1,5},{5... | collective-permute-start | bytes 1572872 | tf_op jit(solution)/shard_map/ppermute | solution.py:435
  98.5 17.7 %collective-permute-start.27 = (bf16[1,2,1024,128]{3,2,1,0:T(8,128)(2,1)S(1)}, bf16[1,2,1024,128]{3,2,1,0:T(8,128)(2,1)S(1)}, u32[]{:S(2)}, u32[]{:S(2)}) collective-permute-start(bf16[1,2,1024,128]{3,2,1,0:T(8,128)(2,1)S(1)} %collective-permute-done.23.refs_18_), channel_id=1, source_target_pairs={{0,4},{4,0},{8,12},{12,8},{16,20},{20,16},{24,28},{28,24},{1,5},{5... | collective-permute-start | bytes 1572872 | tf_op jit(solution)/shard_map/ppermute | solution.py:435
  98.5 18.2 %collective-permute-start.4 = (bf16[256,1024]{1,0:T(8,128)(2,1)S(1)}, bf16[256,1024]{1,0:T(8,128)(2,1)S(1)}, u32[]{:S(2)}, u32[]{:S(2)}) collective-permute-start(bf16[256,1024]{1,0:T(8,128)(2,1)S(1)} %get-tuple-element.29), channel_id=1, source_target_pairs={{0,1},{1,2},{2,3},{3,4},{4,5},{5,6},{6,7},{7,8},{8,9},{9,10},{10,1... | collective-permute-start | bytes 1572872 | tf_op jit(solution)/shard_map/ppermute | solution.py:453
  103.5 23.9 %collective-permute-start.5 = (bf16[256,1024]{1,0:T(8,128)(2,1)S(1)}, bf16[256,1024]{1,0:T(8,128)(2,1)S(1)}, u32[]{:S(2)}, u32[]{:S(2)}) collective-permute-start(bf16[256,1024]{1,0:T(8,128)(2,1)S(1)} %get-tuple-element.30), channel_id=1, source_target_pairs={{1,0},{2,1},{3,2},{4,3},{5,4},{6,5},{7,6},{8,7},{9,8},{10,9},{11,1... | collective-permute-start | bytes 1572872 | tf_op jit(solution)/shard_map/ppermute | solution.py:454
  113.8 24.9 %collective-permute-start.32 = (bf16[1,2,1024,128]{3,2,1,0:T(8,128)(2,1)S(1)}, bf16[1,2,1024,128]{3,2,1,0:T(8,128)(2,1)S(1)}, u32[]{:S(2)}, u32[]{:S(2)}) collective-permute-start(bf16[1,2,1024,128]{3,2,1,0:T(8,128)(2,1)S(1)} %broadcast_select_fusion.refs_0_), channel_id=1, source_target_pairs={{0,8},{4,12},{8,0},{12,4},{16,24},{20,28},{24,16},{28,20},{1,9},{5... | collective-permute-start | bytes 1572872 | tf_op jit(solution)/shard_map/ppermute | solution.py:434
  116.2 22.4 %collective-permute-start.12 = (bf16[1,2,1024,128]{3,2,1,0:T(8,128)(2,1)S(1)}, bf16[1,2,1024,128]{3,2,1,0:T(8,128)(2,1)S(1)}, u32[]{:S(2)}, u32[]{:S(2)}) collective-permute-start(bf16[1,2,1024,128]{3,2,1,0:T(8,128)(2,1)S(1)} %collective-permute-done.8.refs_3_), channel_id=1, source_target_pairs={{0,4},{4,0},{8,12},{12,8},{16,20},{20,16},{24,28},{28,24},{1,5},{5... | collective-permute-start | bytes 1572872 | tf_op jit(solution)/shard_map/ppermute | solution.py:435
  116.2 23.0 %collective-permute-start.20 = (bf16[1,2,1024,128]{3,2,1,0:T(8,128)(2,1)S(1)}, bf16[1,2,1024,128]{3,2,1,0:T(8,128)(2,1)S(1)}, u32[]{:S(2)}, u32[]{:S(2)}) collective-permute-start(bf16[1,2,1024,128]{3,2,1,0:T(8,128)(2,1)S(1)} %collective-permute-done.16.refs_11_), channel_id=1, source_target_pairs={{0,4},{4,0},{8,12},{12,8},{16,20},{20,16},{24,28},{28,24},{1,5},{5... | collective-permute-start | bytes 1572872 | tf_op jit(solution)/shard_map/ppermute | solution.py:435
  116.7 24.6 %collective-permute-start.28 = (bf16[1,2,1024,128]{3,2,1,0:T(8,128)(2,1)S(1)}, bf16[1,2,1024,128]{3,2,1,0:T(8,128)(2,1)S(1)}, u32[]{:S(2)}, u32[]{:S(2)}) collective-permute-start(bf16[1,2,1024,128]{3,2,1,0:T(8,128)(2,1)S(1)} %collective-permute-done.24.refs_19_), channel_id=1, source_target_pairs={{0,4},{4,0},{8,12},{12,8},{16,20},{20,16},{24,28},{28,24},{1,5},{5... | collective-permute-start | bytes 1572872 | tf_op jit(solution)/shard_map/ppermute | solution.py:435
  (25 other events, 361.0 us)
